TPU v7x, 128 devices: a whole 4x4x4 slice. The times are simulated.
128 devices in a mesh: grp: 4 (over x), orient: 32 (over y, z, core).
Axes of the slice: x: 4, y: 4, z: 4, core: 2. Of those that a mesh axis runs over, the one named last changes fastest.
Arguments:
- images: bfloat16 [4096, 2, 8192], P(('grp', 'orient')), may hold values from -6 to 6
- ctf: bfloat16 [4096, 8192], P(('grp', 'orient')), may hold values from -1 to 1
- shifts: int32 [4096, 2], P(('grp', 'orient')), may hold values from -8 to 8
- home: int32 [4, 4096, 1], P(None, ('grp', 'orient')), may hold values from 0 to 31; in each aligned block of 32 rows (0 to 31, 32 to 63, ..., all dimensions but the last counted through in order) at most 2 rows name the same one
- neighbours: int32 [4096, 4, 128], P(('grp', 'orient')), may hold values from 0 to 511
- references: bfloat16 [4, 16384, 2, 8192], P('grp', 'orient'), may hold values from -6 to 6
- noise_weight: float32 [4, 8192], P('grp'), may hold values from 0.25 to 4
Outputs:
- centred: float32 [4096, 4, 128], P(('grp', 'orient'))
Inputs may be any that keep to these rules, and one draw needn't show every extreme that they name: `home`: within one group, at most 2 of the 32 particles of one device share a block, and in every draw some device has exactly 2 particles in one block.
All inputs are finite; a program needn't handle non-finite values.
Results may differ from a plain program's by a relative error of at most 0.0042.
Values may be sent and summed in bfloat16 or wider, within the bound.
No kernel may reach another device: no remote copies, remote signals or barrier semaphores. Data moves between devices by JAX's collectives and lax.ppermute only.
A program may use at most 256 MiB of HBM per device.

v0:
```python
import math

import jax
import jax.numpy as jnp
from jax import lax
from jax.sharding import PartitionSpec as P

BOX = 128
PIX = 8192


def shift_tables(shifts, box):
    half = box // 2
    row = jnp.arange(box, dtype=jnp.int32)
    freq_y = jnp.where(row < half, row, row - box).astype(jnp.float32)
    freq_x = jnp.arange(half, dtype=jnp.int32).astype(jnp.float32)
    grid_y = jnp.broadcast_to(freq_y[:, None], (box, half)).reshape(-1)
    grid_x = jnp.broadcast_to(freq_x[None, :], (box, half)).reshape(-1)
    move_x = shifts[:, 0].astype(jnp.float32)
    move_y = shifts[:, 1].astype(jnp.float32)
    angle = (
        -2.0
        * math.pi
        / box
        * (move_x[:, None] * grid_x[None, :] + move_y[:, None] * grid_y[None, :])
    )
    return (jnp.cos(angle), jnp.sin(angle))


def pick_columns(table, lists):
    width = table.shape[-1]
    marks = (lists[..., None] == jnp.arange(width, dtype=jnp.int32)).astype(jnp.float32)
    return jnp.einsum("ano,ao->an", marks, table, precision=lax.Precision.HIGHEST)


def per_device(images, ctf, shifts, home, neighbours, references, noise_weight):
    groups = home.shape[0]
    owners = lax.axis_size("orient")
    devices = groups * owners
    local = images.shape[0]
    pixels = images.shape[2]
    slots = max(2, 2 * local // owners)
    cosine, sine = shift_tables(shifts, BOX)
    real = images[:, 0].astype(jnp.float32)
    imag = images[:, 1].astype(jnp.float32)
    payload = jnp.stack(
        [real * cosine - imag * sine, real * sine + imag * cosine, ctf.astype(jnp.float32)], axis=1
    ).astype(jnp.bfloat16)
    target = home[:, :, 0]
    places = jnp.arange(owners, dtype=jnp.int32)
    hits = (target[:, :, None] == places[None, None, :]).astype(jnp.int32)
    rank = jnp.sum((jnp.cumsum(hits, axis=1) - hits) * hits, axis=2)
    slot = (jnp.arange(groups, dtype=jnp.int32)[:, None] * owners + target) * slots + rank
    total = devices * slots
    chosen = (slot[:, None, :] == jnp.arange(total, dtype=jnp.int32)[None, :, None]).astype(
        jnp.int32
    )
    select = jnp.sum(chosen, axis=0).astype(jnp.bfloat16)
    buffer = jnp.dot(select, payload.reshape(local, -1), preferred_element_type=jnp.float32).astype(
        jnp.bfloat16
    )
    buffer = buffer.reshape(devices, slots, 3, pixels)
    weight = noise_weight[0]
    blocks = references[0]
    flat_refs = blocks.reshape(blocks.shape[0], -1)
    ref_real = blocks[:, 0].astype(jnp.float32)
    ref_imag = blocks[:, 1].astype(jnp.float32)
    ref_power = (ref_real * ref_real + ref_imag * ref_imag).astype(jnp.bfloat16)
    scale = 1.0 / math.sqrt(PIX)
    contract = (((1,), (1,)), ((), ()))
    arrived = lax.all_to_all(buffer, ("grp", "orient"), split_axis=0, concat_axis=0, tiled=True)
    lead = arrived.shape[:2]
    flat = arrived.reshape(-1, 3, pixels).astype(jnp.float32)
    tone = weight[None, :] * flat[:, 2]
    weighted = (tone[:, None, :] * flat[:, :2]).astype(jnp.bfloat16).reshape(flat.shape[0], -1)
    tone_power = (tone * flat[:, 2]).astype(jnp.bfloat16)
    cross = lax.dot_general(weighted, flat_refs, contract, preferred_element_type=jnp.float32)
    power = lax.dot_general(tone_power, ref_power, contract, preferred_element_type=jnp.float32)
    table = ((power - 2.0 * cross) * scale).reshape(lead + (-1,))
    returned = lax.all_to_all(table, ("grp", "orient"), split_axis=0, concat_axis=0, tiled=True)
    flat_back = returned.reshape(total, -1)
    mine = jnp.einsum(
        "gsp,sk->pgk", chosen.astype(jnp.float32), flat_back, precision=lax.Precision.HIGHEST
    )
    mine = pick_columns(
        mine.reshape(local * groups, -1), neighbours.reshape(local * groups, -1)
    ).reshape(local, groups, -1)
    return mine - jnp.mean(mine, axis=2, keepdims=True)


def solution(mesh):
    in_specs = (
        P(("grp", "orient"), None, None),
        P(("grp", "orient"), None),
        P(("grp", "orient"), None),
        P(None, ("grp", "orient"), None),
        P(("grp", "orient"), None, None),
        P("grp", "orient", None, None),
        P("grp", None),
    )
    out_specs = P(("grp", "orient"), None, None)
    return jax.shard_map(
        per_device, mesh=mesh, in_specs=in_specs, out_specs=out_specs, check_vma=False
    )
```

profile of v0, /device:TPU:1, one launch (start us, length us, event | category | flops | bytes accessed | tf_op | source)
XLA Modules:
  0.0 425.9 jit_solution(6281003190548048576)
XLA Ops:
  0.0 3.7 fusion.31
  3.7 0.8 convert_bitcast_fusion.1
  4.7 4.8 %fusion.23 = (bf16[32,1,8192]{2,0,1:T(8,128)(2,1)S(1)}, bf16[32,1,8192]{2,0,1:T(8,128)(2,1)S(1)}) fusion(f32[8192]{0:T(1024)S(1)} %mul.160, f32[32]{0:T(128)S(1)} %get-tuple-element.10, f32[8192]{0:T(1024)S(1)} %mul.156, f32[32]{0:T(128)S(1)} %get-tuple-element.9, bf16[32,1,8192]{2,1,0:T(2,128)(2,1)S(1)} %get-tuple-element.8, ...), kind=kLoop, calls=%fused_computation.27 | loop fusion | flops 3670016 | bytes 2162944 | tf_op jit(solution)/shard_map/convert.2
  9.5 1.2 maximum_bitcast_fusion
  10.7 0.1 copy.52
  11.0 0.2 select_reduce_fusion
  11.4 6.3 %convolution_convert_fusion = bf16[256,24576]{1,0:T(8,128)(2,1)} fusion(bf16[32,24576]{1,0:T(8,128)(2,1)S(1)} %bitcast.56, s32[256,32]{0,1:T(8,128)S(1)} %convert_reduce_fusion), kind=kOutput, calls=%fused_computation.2 | convolution fusion | flops 408952832 | bytes 14188544 | tf_op jit(solution)/shard_map/dot_general | solution.py:59
  17.7 30.0 %reshape.315 = bf16[128,2,3,8192]{3,2,1,0:T(4,128)(2,1)} reshape(bf16[256,24576]{1,0:T(8,128)(2,1)} %convolution_convert_fusion) | data formatting | bytes 25165824 | tf_op jit(solution)/shard_map/reshape | solution.py:62
  47.7 24.7 %copy.42 = bf16[128,2,3,8192]{3,1,2,0:T(2,128)(2,1)} copy(bf16[128,2,3,8192]{3,2,1,0:T(4,128)(2,1)} %reshape.315) | data formatting | bytes 25165824 | tf_op jit(solution)/shard_map/reshape | solution.py:62
  72.3 11.9 %all-to-all-start = ((bf16[128,2,3,8192]{3,1,2,0:T(2,128)(2,1)}), bf16[128,2,3,8192]{3,1,2,0:T(2,128)(2,1)}, u32[]{:S(2)}, u32[]{:S(2)}) async-start(bf16[128,2,3,8192]{3,1,2,0:T(2,128)(2,1)} %copy.42), calls=%async_computation | async-start | bytes 25165824 | tf_op jit(solution)/shard_map/all_to_all | solution.py:71
  84.3 18.5 %copy.60 = bf16[1,512,2,8192]{3,1,2,0:T(8,128)(2,1)} copy(bf16[1,512,2,8192]{3,2,1,0:T(2,128)(2,1)} %param.12) | data formatting | bytes 33554432 | tf_op args[5]
  102.8 18.5 %copy.53 = bf16[64,8,2,8192]{3,1,2,0:T(8,128)(2,1)} copy(bf16[64,8,2,8192]{3,2,1,0:T(2,128)(2,1)} %bitcast.52) | data formatting | bytes 33554432
  121.3 123.8 %all-to-all-done = bf16[128,2,3,8192]{3,1,2,0:T(2,128)(2,1)} async-done(((bf16[128,2,3,8192]{3,1,2,0:T(2,128)(2,1)}), bf16[128,2,3,8192]{3,1,2,0:T(2,128)(2,1)}, u32[]{:S(2)}, u32[]{:S(2)}) %all-to-all-start) | async-done | bytes 12582944 | tf_op jit(solution)/shard_map/all_to_all | solution.py:71
  245.1 17.8 %copy_convert_fusion = f32[128,2,3,8192]{3,0,2,1:T(8,128)} fusion(bf16[128,2,3,8192]{3,1,2,0:T(2,128)(2,1)} %all-to-all-done), kind=kLoop, calls=%fused_computation.8 | loop fusion | flops 6291456 | bytes 37748736 | tf_op jit(solution)/shard_map/convert_element_type | solution.py:73
  262.9 41.9 %copy.44 = f32[128,2,3,8192]{3,1,0,2:T(2,128)} copy(f32[128,2,3,8192]{3,0,2,1:T(8,128)} %copy_convert_fusion) | data formatting | bytes 50331648 | tf_op jit(solution)/shard_map/convert_element_type | solution.py:73
  304.8 30.1 %reshape.321 = f32[256,3,8192]{2,0,1:T(8,128)} reshape(f32[128,2,3,8192]{3,1,0,2:T(2,128)} %copy.44) | data formatting | bytes 50331648 | tf_op jit(solution)/shard_map/convert_element_type | solution.py:73
  334.9 4.3 %multiply_bitcast_fusion = f32[256,8192]{1,0:T(8,128)S(1)} fusion(f32[256,3,8192]{2,0,1:T(8,128)} %reshape.321, f32[8192]{0:T(1024)S(1)} %bitcast.62), kind=kLoop, calls=%fused_computation.9 | loop fusion | flops 2097152 | bytes 16809984 | tf_op jit(solution)/shard_map/mul | solution.py:75
  339.3 9.2 %fusion.1 = bf16[256,2,8192]{2,0,1:T(8,128)(2,1)} fusion(f32[256,3,8192]{2,0,1:T(8,128)} %reshape.321, f32[256,8192]{1,0:T(8,128)S(1)} %multiply_bitcast_fusion), kind=kLoop, calls=%fused_computation.4 | loop fusion | flops 8388608 | bytes 33554432 | tf_op jit(solution)/shard_map/convert_element_type | solution.py:75
  348.5 11.9 %copy.46 = bf16[256,2,8192]{0,2,1:T(8,128)(2,1)} copy(bf16[256,2,8192]{2,0,1:T(8,128)(2,1)} %fusion.1) | data formatting | bytes 16777216 | tf_op jit(solution)/shard_map/convert_element_type | solution.py:75
  360.4 10.6 %convolution_multiply_fusion = f32[256,512]{1,0:T(8,128)S(1)} fusion(bf16[256,16384]{0,1:T(8,128)(2,1)} %bitcast.55, bf16[512,16384]{1,0:T(8,128)(2,1)} %bitcast.54), kind=kOutput, calls=%fused_computation.23 | convolution fusion | flops 4295098368 | bytes 25690112 | tf_op jit(solution)/shard_map/dot_general | solution.py:77
  371.0 10.9 %fusion.17 = f32[256,512]{1,0:T(8,128)S(1)} fusion(f32[256,512]{1,0:T(8,128)S(1)} %convolution_multiply_fusion, bf16[512,2,8192]{2,0,1:T(8,128)(2,1)} %bitcast.53, f32[256,3,8192]{2,0,1:T(8,128)} %reshape.321, f32[8192]{0:T(1024)S(1)} %bitcast.63), kind=kOutput, calls=%fused_computation.25 | convolution fusion | flops 2179203072 | bytes 26247168 | tf_op jit(solution)/shard_map/dot_general | solution.py:78
  381.9 1.1 reshape.317
  383.0 10.9 %all-to-all-start.1 = ((f32[128,2,512]{2,1,0:T(2,128)}), f32[128,2,512]{2,1,0:T(2,128)S(1)}, u32[]{:S(2)}, u32[]{:S(2)}) async-start(f32[128,2,512]{2,1,0:T(2,128)} %reshape.317), calls=%async_computation.1 | async-start | bytes 1048576 | tf_op jit(solution)/shard_map/all_to_all | solution.py:80
  394.0 13.5 %all-to-all-done.1 = f32[128,2,512]{2,1,0:T(2,128)S(1)} async-done(((f32[128,2,512]{2,1,0:T(2,128)}), f32[128,2,512]{2,1,0:T(2,128)S(1)}, u32[]{:S(2)}, u32[]{:S(2)}) %all-to-all-start.1) | async-done | bytes 524320 | tf_op jit(solution)/shard_map/all_to_all | solution.py:80
  407.4 0.4 reshape.318
  407.8 0.4 fusion.32
  408.2 0.2 copy.47
  408.4 0.4 reshape.327
  408.8 16.1 %fusion = f32[128,1,128]{2,1,0:T(1,128)S(1)} fusion(f32[128,512,1]{1,2,0:T(1,128)S(1)} %reshape.327, s32[128,128]{1,0:T(8,128)S(1)} %bitcast.67), kind=kOutput, calls=%fused_computation.1 | convolution fusion | flops 109051904 | bytes 393216 | tf_op jit(solution)/shard_map/ano,ao->an/dot_general | solution.py:33
  424.9 0.1 reduce_sum.29
  425.0 0.1 div.10
  425.1 0.7 broadcast_subtract_fusion
  (19 shorter events, 0.7 us)
Async XLA Ops:
  0.0 10.8 %copy-start.1 = (s32[4,32,1]{1,2,0:T(1,128)S(1)}, s32[4,32,1]{1,2,0:T(1,128)}, u32[]{:S(2)}) copy-start(s32[4,32,1]{1,2,0:T(1,128)} %param.10) | copy-start | bytes 1540
  72.3 172.7 %all-to-all-start = ((bf16[128,2,3,8192]{3,1,2,0:T(2,128)(2,1)}), bf16[128,2,3,8192]{3,1,2,0:T(2,128)(2,1)}, u32[]{:S(2)}, u32[]{:S(2)}) async-start(bf16[128,2,3,8192]{3,1,2,0:T(2,128)(2,1)} %copy.42), calls=%async_computation | async-start | bytes 25165824 | tf_op jit(solution)/shard_map/all_to_all | solution.py:71
  304.8 30.1 %copy-start = (f32[1,8192]{1,0:T(1,128)S(1)}, f32[1,8192]{1,0:T(1,128)}, u32[]{:S(2)}) copy-start(f32[1,8192]{1,0:T(1,128)} %param.13) | copy-start | bytes 98308
  371.0 37.7 %copy-start.2 = (s32[32,4,128]{2,1,0:T(4,128)S(1)}, s32[32,4,128]{2,1,0:T(4,128)}, u32[]{:S(2)}) copy-start(s32[32,4,128]{2,1,0:T(4,128)} %param.11) | copy-start | bytes 196612
  383.0 24.4 %all-to-all-start.1 = ((f32[128,2,512]{2,1,0:T(2,128)}), f32[128,2,512]{2,1,0:T(2,128)S(1)}, u32[]{:S(2)}, u32[]{:S(2)}) async-start(f32[128,2,512]{2,1,0:T(2,128)} %reshape.317), calls=%async_computation.1 | async-start | bytes 1048576 | tf_op jit(solution)/shard_map/all_to_all | solution.py:80
where the time goes:
time: 429 us; the launch traced here: 426 us
  local copies, waits for them, and re-layouts  182 us (42%)
  waiting for transfers between devices  137 us (32%)
  matrix products  44.3 us (10%)
  other arithmetic  39.6 us (9%)
  starting transfers between devices  22.8 us (5%)
    all_to_all x1, waiting for transfers between devices, per_device(): lax.all_to_all(buffer, ('grp', 'orient'), split_axis=0, concat_axis=0, ti...  124 us
    convert_element_type x2, local copies, waits for them, and re-layouts, per_device(): flat = arrived.reshape(-1, 3, pixels).astype(jnp.float32)  72 us
    reshape x2, local copies, waits for them, and re-layouts, per_device(): buffer = buffer.reshape(devices, slots, 3, pixels)  54.6 us
    unnamed x8, local copies, waits for them, and re-layouts  37 us
    convert_element_type x1, other arithmetic, per_device(): flat = arrived.reshape(-1, 3, pixels).astype(jnp.float32)  17.8 us
    dot_general x1, matrix products, pick_columns(): jnp.einsum('ano,ao->an', marks, table, precision=lax.Precision.HIGHEST)  16.1 us
    all_to_all x1, waiting for transfers between devices, per_device(): lax.all_to_all(table, ('grp', 'orient'), split_axis=0, concat_axis=0, til...  13.5 us
    convert_element_type x1, local copies, waits for them, and re-layouts, per_device(): (tone[:, None, :] * flat[:, :2]).astype(jnp.bfloat16)  11.9 us
  transfers between devices with their start and end apart: 2, of which 2 were waited for; matrix products, arithmetic and copies ran while one was open for 9% of the time, Pallas kernels for 0%

commit v1 on v0

v1 whole, which is shorter than its diff:
```python
import math

import jax
import jax.numpy as jnp
from jax import lax
from jax.experimental import pallas as pl
from jax.experimental.pallas import tpu as pltpu
from jax.sharding import PartitionSpec as P

BOX = 128
PIX = 8192
LANES = 128
SLABS = PIX // LANES
CHUNKS = 2
GROUP = 8


def rotation(move_x, move_y, slab):
    lane = lax.broadcasted_iota(jnp.int32, move_x.shape, 1)
    row = 2 * slab + jnp.where(lane >= 64, 1, 0) - jnp.where(slab >= SLABS // 2, BOX, 0)
    turns = move_x * (lane & 63).astype(jnp.float32) + move_y * row.astype(jnp.float32)
    quarter = jnp.round(turns * (1.0 / 32.0))
    phi = (turns - 32.0 * quarter) * (2.0 * math.pi / BOX)
    sq = phi * phi
    sine = phi * (1.0 + sq * (-1.0 / 6 + sq * (1.0 / 120 + sq * (-1.0 / 5040 + sq * (1.0 / 362880)))))
    cosine = 1.0 + sq * (-0.5 + sq * (1.0 / 24 + sq * (-1.0 / 720 + sq * (1.0 / 40320))))
    step = quarter.astype(jnp.int32) & 3
    swap = (step & 1) == 1
    base_c = jnp.where(swap, sine, cosine)
    base_s = jnp.where(swap, cosine, sine)
    return (
        jnp.where((step == 1) | (step == 2), -base_c, base_c),
        jnp.where(step >= 2, -base_s, base_s),
    )


def pack_kernel(chunk, width, shift_ref, select_ref, real_ref, imag_ref, ctf_ref, out_ref):
    local = shift_ref.shape[0]
    devices, _, slots, _ = out_ref.shape
    move_x = jnp.broadcast_to(shift_ref[:, 0:1].astype(jnp.float32), (local, LANES))
    move_y = jnp.broadcast_to(shift_ref[:, 1:2].astype(jnp.float32), (local, LANES))

    def one(r, carry):
        cols = pl.ds(pl.multiple_of(r * LANES, LANES), LANES)
        cosine, sine = rotation(move_x, move_y, chunk * width + r)
        real = real_ref[:, cols].astype(jnp.float32)
        imag = imag_ref[:, cols].astype(jnp.float32)
        payload = jnp.concatenate(
            [
                (real * cosine + imag * sine).astype(jnp.bfloat16),
                (imag * cosine - real * sine).astype(jnp.bfloat16),
                ctf_ref[:, cols],
            ],
            axis=1,
        )
        packed = jnp.dot(
            select_ref[...], payload, preferred_element_type=jnp.float32
        ).astype(jnp.bfloat16)
        for part in range(3):
            piece = packed[:, part * LANES : (part + 1) * LANES]
            out_ref[:, part * width + r] = piece.reshape(devices, slots, LANES)
        return carry

    lax.fori_loop(0, width, one, 0, unroll=2)


def pack(chunk, shifts, select, real, imag, ctf, devices, slots):
    local = shifts.shape[0]
    width = SLABS // CHUNKS
    block = pl.BlockSpec((local, width * LANES), lambda i: (0, chunk))
    whole = lambda array: pl.BlockSpec(array.shape, lambda i: (0, 0))
    shape = (devices, 3 * width, slots, LANES)

    def body(*refs):
        pack_kernel(chunk, width, *refs)

    return pl.pallas_call(
        body,
        grid=(1,),
        in_specs=[whole(shifts), whole(select), block, block, block],
        out_specs=pl.BlockSpec(shape, lambda i: (0, 0, 0, 0)),
        out_shape=jax.ShapeDtypeStruct(shape, jnp.bfloat16),
        cost_estimate=pl.CostEstimate(
            flops=2 * devices * slots * local * 3 * width * LANES,
            bytes_accessed=2 * 3 * width * LANES * (devices * slots + local),
            transcendentals=0,
        ),
        compiler_params=pltpu.CompilerParams(vmem_limit_bytes=48 * 2**20),
        name=f"pack_{chunk}",
    )(shifts, select, real, imag, ctf)


def match_kernel(arrived_ref, base_ref, weight_ref, re_ref, im_ref, pw_ref, out_ref):
    @pl.when(pl.program_id(0) == 0)
    def _():
        out_ref[...] = base_ref[...]

    rows = out_ref.shape[0]
    sides = ([], [], [])
    for r in range(GROUP):
        real, imag, ctf = (
            arrived_ref[:, part, r].reshape(rows, LANES).astype(jnp.float32) for part in range(3)
        )
        tone = ctf * weight_ref[:, r * LANES : (r + 1) * LANES]
        for side, value in zip(sides, (real, imag, ctf)):
            side.append((tone * value).astype(jnp.bfloat16))
    contract = (((1,), (1,)), ((), ()))
    scale = 1.0 / math.sqrt(PIX)
    cross = lax.dot_general(
        jnp.concatenate(sides[0], axis=1), re_ref[...], contract, preferred_element_type=jnp.float32
    ) + lax.dot_general(
        jnp.concatenate(sides[1], axis=1), im_ref[...], contract, preferred_element_type=jnp.float32
    )
    power = lax.dot_general(
        jnp.concatenate(sides[2], axis=1), pw_ref[...], contract, preferred_element_type=jnp.float32
    )
    out_ref[...] += (power - 2.0 * cross) * scale


def match(chunk, arrived, base, weight, tables):
    devices, depth, slots, _ = arrived.shape
    width = depth // 3
    steps = width // GROUP
    orients = tables[0].shape[0]
    arrived = arrived.reshape(devices, 3, width, slots, LANES)
    table = pl.BlockSpec((orients, GROUP * LANES), lambda i: (0, chunk * steps + i))
    full = pl.BlockSpec((devices * slots, orients), lambda i: (0, 0))
    return pl.pallas_call(
        match_kernel,
        grid=(steps,),
        in_specs=[
            pl.BlockSpec((devices, 3, GROUP, slots, LANES), lambda i: (0, 0, i, 0, 0)),
            full,
            pl.BlockSpec((1, GROUP * LANES), lambda i: (0, chunk * steps + i)),
            table,
            table,
            table,
        ],
        out_specs=full,
        out_shape=jax.ShapeDtypeStruct((devices * slots, orients), jnp.float32),
        cost_estimate=pl.CostEstimate(
            flops=2 * devices * slots * orients * depth * LANES,
            bytes_accessed=2 * depth * LANES * (devices * slots + orients),
            transcendentals=0,
        ),
        compiler_params=pltpu.CompilerParams(vmem_limit_bytes=48 * 2**20),
        name=f"match_{chunk}",
    )(arrived, base, weight, *tables)


def pick_kernel(rows_ref, near_ref, out_ref):
    near = near_ref[...]
    lane = near & (LANES - 1)
    band = near // LANES
    picked = jnp.zeros(near.shape, jnp.float32)
    for at in range(rows_ref.shape[1] // LANES):
        piece = rows_ref[:, at * LANES : (at + 1) * LANES]
        found = jnp.take_along_axis(piece, lane, axis=1)
        picked = jnp.where(band == at, found, picked)
    out_ref[...] = picked - jnp.mean(picked, axis=1, keepdims=True)


def pick(rows, near):
    return pl.pallas_call(
        pick_kernel,
        out_shape=jax.ShapeDtypeStruct(near.shape, jnp.float32),
        name="pick",
    )(rows, near)


def per_device(images, ctf, shifts, home, neighbours, references, noise_weight):
    groups = home.shape[0]
    owners = lax.axis_size("orient")
    devices = groups * owners
    local = images.shape[0]
    slots = max(2, 2 * local // owners)
    total = devices * slots
    target = home[:, :, 0]
    earlier = jnp.arange(local)[:, None] > jnp.arange(local)[None, :]
    same = target[:, :, None] == target[:, None, :]
    rank = jnp.sum((same & earlier[None]).astype(jnp.int32), axis=2)
    slot = (jnp.arange(groups, dtype=jnp.int32)[:, None] * owners + target) * slots + rank
    select = jnp.sum(
        (slot[:, None, :] == jnp.arange(total, dtype=jnp.int32)[None, :, None]).astype(jnp.int32),
        axis=0,
    ).astype(jnp.bfloat16)
    real, imag = images[:, 0], images[:, 1]
    sent = [pack(c, shifts, select, real, imag, ctf, devices, slots) for c in range(CHUNKS)]
    arrived = [
        lax.all_to_all(s, ("grp", "orient"), split_axis=0, concat_axis=0, tiled=True) for s in sent
    ]
    ref_real, ref_imag = references[0, :, 0], references[0, :, 1]
    wide_real, wide_imag = ref_real.astype(jnp.float32), ref_imag.astype(jnp.float32)
    ref_power = (wide_real * wide_real + wide_imag * wide_imag).astype(jnp.bfloat16)
    tables = (ref_real, ref_imag, ref_power)
    score = jnp.zeros((total, references.shape[1]), jnp.float32)
    for c in range(CHUNKS):
        score = match(c, arrived[c], score, noise_weight, tables)
    returned = lax.all_to_all(
        score.reshape(devices, slots, -1), ("grp", "orient"), split_axis=0, concat_axis=0, tiled=True
    )
    flat_back = returned.reshape(total, -1)
    chosen = (
        slot.T.reshape(-1)[:, None] == jnp.arange(total, dtype=jnp.int32)[None, :]
    ).astype(jnp.float32)
    mine = jnp.dot(chosen, flat_back, precision=lax.Precision.HIGHEST)
    return pick(mine, neighbours.reshape(local * groups, -1)).reshape(local, groups, -1)


def solution(mesh):
    in_specs = (
        P(("grp", "orient"), None, None),
        P(("grp", "orient"), None),
        P(("grp", "orient"), None),
        P(None, ("grp", "orient"), None),
        P(("grp", "orient"), None, None),
        P("grp", "orient", None, None),
        P("grp", None),
    )
    out_specs = P(("grp", "orient"), None, None)
    return jax.shard_map(
        per_device, mesh=mesh, in_specs=in_specs, out_specs=out_specs, check_vma=False
    )
```

time: 429 us -> 239 us (0.56)
  local copies, waits for them, and re-layouts: 182 us -> 49 us
  waiting for transfers between devices: 137 us -> 77.5 us
  Pallas kernels: 0 us -> 46.2 us
  matrix products: 44.3 us -> 1.04 us
  starting transfers between devices: 22.8 us -> 30.9 us
  other arithmetic: 39.6 us -> 33.3 us
    convert_element_type x4 -> x0, local copies, waits for them, and re-layouts: 84.1 us -> none  [the longest x2 72 us: per_device(): flat = arrived.reshape(-1, 3, pixels).astype(jnp.float32)]
    all_to_all x2 -> x3, waiting for transfers between devices: 137 us -> 77.5 us  [the longest x2 64.1 us: per_device(): lax.all_to_all(s, ('grp', 'orient'), split_axis=0, concat_axis=0, tiled=T...]
    reshape x4 -> x1, local copies, waits for them, and re-layouts: 56.1 us -> 1.09 us  [per_device(): score.reshape(devices, slots, -1)]
    pallas_call x0 -> x5, Pallas kernels: none -> 46.2 us  [the longest x2 22.4 us: pack(): pl.pallas_call(body, grid=(1,), in_specs=[whole(shifts), whole(select), b...]
    dot_general x4 -> x1, matrix products: 43.9 us -> 1.04 us  [per_device(): mine = jnp.dot(chosen, flat_back, precision=lax.Precision.HIGHEST)]
    slice x1 -> x2, local copies, waits for them, and re-layouts: 3.68 us -> 43 us  [the longest x1 37.6 us: per_device(): ref_real, ref_imag = (references[0, :, 0], references[0, :, 1])]
    unnamed x8 -> x7, local copies, waits for them, and re-layouts: 37 us -> 1.81 us
    all_to_all x2 -> x3, starting transfers between devices: 22.8 us -> 30.9 us  [the longest x2 21.2 us: per_device(): lax.all_to_all(s, ('grp', 'orient'), split_axis=0, concat_axis=0, tiled=T...]
  transfers between devices with their start and end apart: 2 -> 3, of which waited for: 2 -> 2; matrix products, arithmetic and copies ran while one was open for 9% -> 29% of each run, Pallas kernels for 0% -> 9%
where the time goes in v1:
time: 239 us; the launch traced here: 238 us
  waiting for transfers between devices  77.5 us (32%)
  local copies, waits for them, and re-layouts  49 us (21%)
  Pallas kernels  46.2 us (19%)
  other arithmetic  33.3 us (14%)
  starting transfers between devices  30.9 us (13%)
    all_to_all x2, waiting for transfers between devices, per_device(): lax.all_to_all(s, ('grp', 'orient'), split_axis=0, concat_axis=0, tiled=T...  64.1 us
    slice x1, local copies, waits for them, and re-layouts, per_device(): ref_real, ref_imag = (references[0, :, 0], references[0, :, 1])  37.6 us
    convert_element_type x1, other arithmetic, per_device(): (wide_real * wide_real + wide_imag * wide_imag).astype(jnp.bfloat16)  31.5 us
    pallas_call x2, Pallas kernels, pack(): pl.pallas_call(body, grid=(1,), in_specs=[whole(shifts), whole(select), b...  22.4 us
    pallas_call x2, Pallas kernels, match(): pl.pallas_call(match_kernel, grid=(steps,), in_specs=[pl.BlockSpec((devic...  21.9 us
    all_to_all x2, starting transfers between devices, per_device(): lax.all_to_all(s, ('grp', 'orient'), split_axis=0, concat_axis=0, tiled=T...  21.2 us
    all_to_all x1, waiting for transfers between devices, per_device(): lax.all_to_all(score.reshape(devices, slots, -1), ('grp', 'orient'), spli...  13.3 us
    all_to_all x1, starting transfers between devices, per_device(): lax.all_to_all(score.reshape(devices, slots, -1), ('grp', 'orient'), spli...  9.76 us
  transfers between devices with their start and end apart: 3, of which 2 were waited for; matrix products, arithmetic and copies ran while one was open for 29% of the time, Pallas kernels for 9%

profile of v1, /device:TPU:1, one launch (start us, length us, event | category | flops | bytes accessed | tf_op | source)
XLA Modules:
  0.0 238.1 jit_solution(16638322485288853737)
XLA Ops:
  0.0 0.0 copy-start.1
  0.0 5.5 %fusion.3 = (bf16[32,1,8192]{2,1,0:T(2,128)(2,1)S(1)}, bf16[32,1,8192]{2,1,0:T(2,128)(2,1)}) fusion(bf16[32,2,8192]{2,1,0:T(2,128)(2,1)} %param.7), kind=kLoop, calls=%fused_computation.15 | loop fusion | bytes 2097152 | tf_op jit(solution)/shard_map/slice | solution.py:187
  5.5 1.0 convert_reduce_fusion.1
  6.5 0.8 multiply_add_fusion
  7.2 0.1 convert_reduce_fusion
  7.3 0.1 copy.23
  7.4 0.8 copy.26.refs_0_
  8.2 2.4 copy_bitcast_fusion.2
  10.6 0.0 copy-start
  10.6 1.0 copy-done
  11.6 11.1 %pack_0.1 = bf16[128,96,2,128]{3,2,1,0:T(2,128)(2,1)} custom-call(s32[32,2]{1,0:T(8,128)S(1)} %copy.26.refs_0_, bf16[256,32]{1,0:T(8,128)(2,1)S(1)} %convert_element_type.21.refs_1_, bf16[32,8192]{1,0:T(8,128)(2,1)S(1)} %get-tuple-element.13.refs_2_, bf16[32,8192]{1,0:T(8,128)(2,1)S(1)} %get-tuple-element.12.refs_3_, bf16[32,8192]{1,0:T(8,128)(2,1)S(1)} %copy-done), custom_call_target="tpu_custom_call" | custom-call | flops 201326592 | bytes 7077888 | tf_op jit(solution)/shard_map/pack_0/pallas_call | solution.py:77
  22.7 11.9 %all-to-all-start.1 = ((bf16[128,96,2,128]{3,2,1,0:T(2,128)(2,1)}), bf16[128,96,2,128]{3,2,1,0:T(2,128)(2,1)}, u32[]{:S(2)}, u32[]{:S(2)}) async-start(bf16[128,96,2,128]{3,2,1,0:T(2,128)(2,1)} %pack_0.1), calls=%async_computation.1 | async-start | bytes 12582912 | tf_op jit(solution)/shard_map/all_to_all | solution.py:190
  34.6 0.0 copy-done.1
  34.6 11.3 %pack_1.1 = bf16[128,96,2,128]{3,2,1,0:T(2,128)(2,1)} custom-call(s32[32,2]{1,0:T(8,128)S(1)} %copy.26.refs_0_, bf16[256,32]{1,0:T(8,128)(2,1)S(1)} %convert_element_type.21.refs_1_, bf16[32,8192]{1,0:T(8,128)(2,1)S(1)} %get-tuple-element.13.refs_2_, bf16[32,8192]{1,0:T(8,128)(2,1)S(1)} %get-tuple-element.12.refs_3_, bf16[32,8192]{1,0:T(8,128)(2,1)S(1)} %copy-done.1), custom_call_target="tpu_custom_call" | custom-call | flops 201326592 | bytes 7077888 | tf_op jit(solution)/shard_map/pack_1/pallas_call | solution.py:77
  45.9 64.1 %all-to-all-done.1 = bf16[128,96,2,128]{3,2,1,0:T(2,128)(2,1)} async-done(((bf16[128,96,2,128]{3,2,1,0:T(2,128)(2,1)}), bf16[128,96,2,128]{3,2,1,0:T(2,128)(2,1)}, u32[]{:S(2)}, u32[]{:S(2)}) %all-to-all-start.1) | async-done | bytes 6291488 | tf_op jit(solution)/shard_map/all_to_all | solution.py:190
  110.0 9.3 %all-to-all-start = ((bf16[128,96,2,128]{3,2,1,0:T(2,128)(2,1)}), bf16[128,96,2,128]{3,2,1,0:T(2,128)(2,1)}, u32[]{:S(2)}, u32[]{:S(2)}) async-start(bf16[128,96,2,128]{3,2,1,0:T(2,128)(2,1)} %pack_1.1), calls=%async_computation | async-start | bytes 12582912 | tf_op jit(solution)/shard_map/all_to_all | solution.py:190
  119.3 37.6 %fusion.2 = (bf16[1,512,1,8192]{3,2,1,0:T(2,128)(2,1)S(1)}, bf16[1,512,1,8192]{3,2,1,0:T(2,128)(2,1)}) fusion(bf16[1,512,2,8192]{3,2,1,0:T(2,128)(2,1)} %param.12), kind=kLoop, calls=%fused_computation.14 | loop fusion | bytes 33554432 | tf_op jit(solution)/shard_map/slice | solution.py:192
  156.9 0.0 copy-start.2
  156.9 31.5 %add_convert_fusion = (bf16[512,8192]{1,0:T(8,128)(2,1)}, bf16[512,8192]{1,0:T(8,128)(2,1)}, bf16[512,8192]{1,0:T(8,128)(2,1)}) fusion(bf16[1,512,1,8192]{3,2,1,0:T(2,128)(2,1)} %get-tuple-element.9, bf16[1,512,1,8192]{3,2,1,0:T(2,128)(2,1)S(1)} %get-tuple-element.8), kind=kLoop, calls=%fused_computation | loop fusion | flops 25165824 | bytes 41943040 | tf_op jit(solution)/shard_map/convert_element_type | solution.py:194
  188.4 0.0 copy-done.2
  188.4 10.8 %match_0.1.base_ref = f32[256,512]{1,0:T(8,128)S(1)} custom-call(bf16[128,3,32,2,128]{4,3,2,1,0:T(2,128)(2,1)} %bitcast.5.arrived_ref, f32[256,512]{1,0:T(8,128)S(1)} %broadcast_in_dim.2.base_ref, f32[1,8192]{1,0:T(1,128)S(1)} %copy-done.2, bf16[512,8192]{1,0:T(8,128)(2,1)} %get-tuple-element.7.re_ref, bf16[512,8192]{1,0:T(8,128)(2,1)} %get-tuple-element.6.im_ref, ...), custom_call_target="tpu_custom_call" | custom-call | flops 3221225472 | bytes 18874368 | tf_op jit(solution)/shard_map/match_0/pallas_call | solution.py:128
  199.3 0.0 all-to-all-done
  199.3 11.1 %match_1.1 = f32[256,512]{1,0:T(8,128)S(1)} custom-call(bf16[128,3,32,2,128]{4,3,2,1,0:T(2,128)(2,1)} %bitcast.4.arrived_ref, f32[256,512]{1,0:T(8,128)S(1)} %match_0.1.base_ref, f32[1,8192]{1,0:T(1,128)S(1)} %copy-done.2, bf16[512,8192]{1,0:T(8,128)(2,1)} %get-tuple-element.7.re_ref, bf16[512,8192]{1,0:T(8,128)(2,1)} %get-tuple-element.6.im_ref, ...), custom_call_target="tpu_custom_call" | custom-call | flops 3221225472 | bytes 18874368 | tf_op jit(solution)/shard_map/match_1/pallas_call | solution.py:128
  210.4 1.1 reshape.59
  211.5 9.8 %all-to-all-start.2 = ((f32[128,2,512]{2,1,0:T(2,128)}), f32[128,2,512]{2,1,0:T(2,128)S(1)}, u32[]{:S(2)}, u32[]{:S(2)}) async-start(f32[128,2,512]{2,1,0:T(2,128)} %reshape.59), calls=%async_computation.2 | async-start | bytes 1048576 | tf_op jit(solution)/shard_map/all_to_all | solution.py:199
  221.3 0.1 copy.22
  221.3 0.1 eq.44
  221.4 13.3 %all-to-all-done.2 = f32[128,2,512]{2,1,0:T(2,128)S(1)} async-done(((f32[128,2,512]{2,1,0:T(2,128)}), f32[128,2,512]{2,1,0:T(2,128)S(1)}, u32[]{:S(2)}, u32[]{:S(2)}) %all-to-all-start.2) | async-done | bytes 524320 | tf_op jit(solution)/shard_map/all_to_all | solution.py:199
  234.8 0.4 reshape.60
  235.2 1.0 fusion.rows_ref
  236.2 1.9 pick.1
  (4 shorter events, 0.1 us)
Async XLA Ops:
  0.0 34.6 %copy-start.1 = (bf16[32,8192]{1,0:T(8,128)(2,1)S(1)}, bf16[32,8192]{1,0:T(8,128)(2,1)}, u32[]{:S(2)}) copy-start(bf16[32,8192]{1,0:T(8,128)(2,1)} %refs_4_.3) | copy-start | bytes 1572868
  10.6 1.0 copy-start
  22.7 87.3 %all-to-all-start.1 = ((bf16[128,96,2,128]{3,2,1,0:T(2,128)(2,1)}), bf16[128,96,2,128]{3,2,1,0:T(2,128)(2,1)}, u32[]{:S(2)}, u32[]{:S(2)}) async-start(bf16[128,96,2,128]{3,2,1,0:T(2,128)(2,1)} %pack_0.1), calls=%async_computation.1 | async-start | bytes 12582912 | tf_op jit(solution)/shard_map/all_to_all | solution.py:190
  110.0 89.2 %all-to-all-start = ((bf16[128,96,2,128]{3,2,1,0:T(2,128)(2,1)}), bf16[128,96,2,128]{3,2,1,0:T(2,128)(2,1)}, u32[]{:S(2)}, u32[]{:S(2)}) async-start(bf16[128,96,2,128]{3,2,1,0:T(2,128)(2,1)} %pack_1.1), calls=%async_computation | async-start | bytes 12582912 | tf_op jit(solution)/shard_map/all_to_all | solution.py:190
  156.9 31.5 %copy-start.2 = (f32[1,8192]{1,0:T(1,128)S(1)}, f32[1,8192]{1,0:T(1,128)}, u32[]{:S(2)}) copy-start(f32[1,8192]{1,0:T(1,128)} %weight_ref.3) | copy-start | bytes 98308
  211.5 23.3 %all-to-all-start.2 = ((f32[128,2,512]{2,1,0:T(2,128)}), f32[128,2,512]{2,1,0:T(2,128)S(1)}, u32[]{:S(2)}, u32[]{:S(2)}) async-start(f32[128,2,512]{2,1,0:T(2,128)} %reshape.59), calls=%async_computation.2 | async-start | bytes 1048576 | tf_op jit(solution)/shard_map/all_to_all | solution.py:199

commit v2 on v1

v2 whole, which is shorter than its diff:
```python
import math

import jax
import jax.numpy as jnp
from jax import lax
from jax.experimental import pallas as pl
from jax.experimental.pallas import tpu as pltpu
from jax.sharding import PartitionSpec as P

BOX = 128
PIX = 8192
LANES = 128
SLABS = PIX // LANES
CHUNKS = 2
GROUP = 8
NEAR = 128


def rotation(move_x, move_y, slab):
    lane = lax.broadcasted_iota(jnp.int32, move_x.shape, 1)
    row = 2 * slab + jnp.where(lane >= 64, 1, 0) - jnp.where(slab >= SLABS // 2, BOX, 0)
    turns = move_x * (lane & 63).astype(jnp.float32) + move_y * row.astype(jnp.float32)
    quarter = jnp.round(turns * (1.0 / 32.0))
    phi = (turns - 32.0 * quarter) * (2.0 * math.pi / BOX)
    sq = phi * phi
    sine = phi * (1.0 + sq * (-1.0 / 6 + sq * (1.0 / 120 + sq * (-1.0 / 5040 + sq * (1.0 / 362880)))))
    cosine = 1.0 + sq * (-0.5 + sq * (1.0 / 24 + sq * (-1.0 / 720 + sq * (1.0 / 40320))))
    step = quarter.astype(jnp.int32) & 3
    swap = (step & 1) == 1
    base_c = jnp.where(swap, sine, cosine)
    base_s = jnp.where(swap, cosine, sine)
    return (
        jnp.where((step == 1) | (step == 2), -base_c, base_c),
        jnp.where(step >= 2, -base_s, base_s),
    )


def pack_kernel(chunk, width, shift_ref, slot_ref, image_ref, ctf_ref, near_ref, out_ref, pair_ref):
    local = shift_ref.shape[0]
    groups = slot_ref.shape[0]
    devices, depth, slots, _ = out_ref.shape
    total = devices * slots
    move_x = jnp.broadcast_to(shift_ref[:, 0:1].astype(jnp.float32), (local, LANES))
    move_y = jnp.broadcast_to(shift_ref[:, 1:2].astype(jnp.float32), (local, LANES))
    place = lax.broadcasted_iota(jnp.int32, (total, local), 0)
    hit = place == slot_ref[0:1, :]
    for g in range(1, groups):
        hit = hit | (place == slot_ref[g : g + 1, :])
    select = jnp.where(hit, 1.0, 0.0).astype(jnp.bfloat16)

    def spread(rows, payload):
        return jnp.dot(rows, payload, preferred_element_type=jnp.float32).astype(jnp.bfloat16)

    def one(r, carry):
        cols = pl.ds(pl.multiple_of(r * LANES, LANES), LANES)
        cosine, sine = rotation(move_x, move_y, chunk * width + r)
        pair_ref[...] = image_ref[:, :, cols].reshape(2 * local, LANES).astype(jnp.float32)
        real = pair_ref[pl.ds(0, local, stride=2), :]
        imag = pair_ref[pl.ds(1, local, stride=2), :]
        payload = jnp.concatenate(
            [
                (real * cosine + imag * sine).astype(jnp.bfloat16),
                (imag * cosine - real * sine).astype(jnp.bfloat16),
                ctf_ref[:, cols],
            ],
            axis=1,
        )
        packed = spread(select, payload)
        for part in range(3):
            piece = packed[:, part * LANES : (part + 1) * LANES]
            out_ref[:, 3 * r + part] = piece.reshape(devices, slots, LANES)
        return carry

    lax.fori_loop(0, width, one, 0, unroll=2)
    if depth > 3 * width:
        share = total // groups
        halves = ([], [])
        for g in range(groups):
            near = near_ref[:, g * NEAR : (g + 1) * NEAR]
            for half, value in zip(halves, (near >> 1, near & 1)):
                half.append(
                    spread(select[g * share : (g + 1) * share], value.astype(jnp.float32).astype(jnp.bfloat16))
                )
        for at, half in enumerate(halves):
            out_ref[:, 3 * width + at] = jnp.concatenate(half, axis=0).reshape(devices, slots, NEAR)


def pack(chunk, shifts, slot, images, ctf, near, devices, slots):
    local = shifts.shape[0]
    width = SLABS // CHUNKS
    span = width * LANES
    depth = 3 * width + (2 if chunk == CHUNKS - 1 else 0)
    whole = lambda array: pl.BlockSpec(array.shape, lambda i: (0, 0))
    shape = (devices, depth, slots, LANES)

    def body(*refs):
        pack_kernel(chunk, width, *refs)

    return pl.pallas_call(
        body,
        grid=(1,),
        in_specs=[
            whole(shifts),
            whole(slot),
            pl.BlockSpec((local, 2, span), lambda i: (0, 0, chunk)),
            pl.BlockSpec((local, span), lambda i: (0, chunk)),
            whole(near),
        ],
        out_specs=pl.BlockSpec(shape, lambda i: (0, 0, 0, 0)),
        out_shape=jax.ShapeDtypeStruct(shape, jnp.bfloat16),
        scratch_shapes=[pltpu.VMEM((2 * local, LANES), jnp.float32)],
        cost_estimate=pl.CostEstimate(
            flops=2 * devices * slots * local * depth * LANES,
            bytes_accessed=2 * depth * LANES * (devices * slots + local),
            transcendentals=0,
        ),
        compiler_params=pltpu.CompilerParams(vmem_limit_bytes=48 * 2**20),
        name=f"pack_{chunk}",
    )(shifts, slot, images, ctf, near)


def table_kernel(block_ref, after_ref, re_ref, im_ref, pw_ref, pair_ref):
    rows, _, span = block_ref.shape

    def one(r, carry):
        cols = pl.ds(pl.multiple_of(r * LANES, LANES), LANES)
        pair_ref[...] = block_ref[:, :, cols].reshape(2 * rows, LANES).astype(jnp.float32)
        real = pair_ref[pl.ds(0, rows, stride=2), :]
        imag = pair_ref[pl.ds(1, rows, stride=2), :]
        re_ref[:, cols] = real.astype(jnp.bfloat16)
        im_ref[:, cols] = imag.astype(jnp.bfloat16)
        pw_ref[:, cols] = (real * real + imag * imag).astype(jnp.bfloat16)
        return carry

    lax.fori_loop(0, span // LANES, one, 0, unroll=4)


def tabulate(blocks, after):
    orients = blocks.shape[0]
    rows = 64
    out = pl.BlockSpec((rows, PIX), lambda i: (i, 0))
    return pl.pallas_call(
        table_kernel,
        grid=(orients // rows,),
        in_specs=[
            pl.BlockSpec((rows, 2, PIX), lambda i: (i, 0, 0)),
            pl.BlockSpec(memory_space=pl.ANY),
        ],
        out_specs=[out] * 3,
        out_shape=[jax.ShapeDtypeStruct((orients, PIX), jnp.bfloat16)] * 3,
        scratch_shapes=[pltpu.VMEM((2 * rows, LANES), jnp.float32)],
        cost_estimate=pl.CostEstimate(
            flops=2 * orients * PIX * 1024, bytes_accessed=10 * orients * PIX, transcendentals=0
        ),
        name="tabulate",
    )(blocks, after)


def accumulate(arrived_ref, weight_ref, re_ref, im_ref, pw_ref, total_ref):
    rows = total_ref.shape[0]
    sides = ([], [], [])
    for r in range(GROUP):
        real, imag, ctf = (
            arrived_ref[:, 3 * r + part].reshape(rows, LANES).astype(jnp.float32)
            for part in range(3)
        )
        tone = ctf * weight_ref[:, r * LANES : (r + 1) * LANES]
        for side, value in zip(sides, (real, imag, ctf)):
            side.append((tone * value).astype(jnp.bfloat16))
    real, imag, power = (
        lax.dot_general(
            jnp.concatenate(side, axis=1),
            table[...],
            (((1,), (1,)), ((), ())),
            preferred_element_type=jnp.float32,
        )
        for side, table in zip(sides, (re_ref, im_ref, pw_ref))
    )
    total_ref[...] += power - 2.0 * (real + imag)


def match_first(arrived_ref, weight_ref, re_ref, im_ref, pw_ref, total_ref):
    @pl.when(pl.program_id(0) == 0)
    def _():
        total_ref[...] = jnp.zeros_like(total_ref)

    accumulate(arrived_ref, weight_ref, re_ref, im_ref, pw_ref, total_ref)


def match_last(
    arrived_ref, weight_ref, re_ref, im_ref, pw_ref, base_ref, near_ref, out_ref, total_ref
):
    @pl.when(pl.program_id(0) == 0)
    def _():
        total_ref[...] = base_ref[...]

    accumulate(arrived_ref, weight_ref, re_ref, im_ref, pw_ref, total_ref)

    @pl.when(pl.program_id(0) == pl.num_programs(0) - 1)
    def _():
        rows = total_ref.shape[0]
        high, low = (
            near_ref[:, at].reshape(rows, NEAR).astype(jnp.float32).astype(jnp.int32)
            for at in range(2)
        )
        near = 2 * high + low
        lane, band = near & (LANES - 1), near >> 7
        picked = jnp.zeros(near.shape, jnp.float32)
        for at in range(total_ref.shape[1] // LANES):
            piece = total_ref[:, at * LANES : (at + 1) * LANES]
            found = jnp.take_along_axis(piece, lane, axis=1)
            picked = jnp.where(band == at, found, picked)
        picked = picked * (1.0 / math.sqrt(PIX))
        picked = picked - jnp.mean(picked, axis=1, keepdims=True)
        out_ref[...] = picked.reshape(out_ref.shape)


def match(chunk, arrived, weight, tables, base=None):
    devices, depth, slots, _ = arrived.shape
    width = SLABS // CHUNKS
    steps = width // GROUP
    orients = tables[0].shape[0]
    rows = devices * slots
    table = pl.BlockSpec((orients, GROUP * LANES), lambda i: (0, chunk * steps + i))
    full = pl.BlockSpec((rows, orients), lambda i: (0, 0))
    in_specs = [
        pl.BlockSpec((devices, 3 * GROUP, slots, LANES), lambda i: (0, i, 0, 0)),
        pl.BlockSpec((1, GROUP * LANES), lambda i: (0, chunk * steps + i)),
        table,
        table,
        table,
    ]
    common = dict(
        grid=(steps,),
        cost_estimate=pl.CostEstimate(
            flops=2 * rows * orients * depth * LANES,
            bytes_accessed=2 * depth * LANES * (rows + orients),
            transcendentals=0,
        ),
        compiler_params=pltpu.CompilerParams(vmem_limit_bytes=48 * 2**20),
        name=f"match_{chunk}",
    )
    if base is None:
        return pl.pallas_call(
            match_first,
            in_specs=in_specs,
            out_specs=full,
            out_shape=jax.ShapeDtypeStruct((rows, orients), jnp.float32),
            **common,
        )(arrived, weight, *tables)
    extra = pl.BlockSpec((devices, 2, slots, LANES), lambda i: (0, 3 * width // 2, 0, 0))
    return pl.pallas_call(
        match_last,
        in_specs=in_specs + [full, extra],
        out_specs=pl.BlockSpec((devices, slots, NEAR), lambda i: (0, 0, 0)),
        out_shape=jax.ShapeDtypeStruct((devices, slots, NEAR), jnp.float32),
        scratch_shapes=[pltpu.VMEM((rows, orients), jnp.float32)],
        **common,
    )(arrived, weight, *tables, base, arrived)


def per_device(images, ctf, shifts, home, neighbours, references, noise_weight):
    groups = home.shape[0]
    owners = lax.axis_size("orient")
    devices = groups * owners
    local = images.shape[0]
    slots = max(2, 2 * local // owners)
    total = devices * slots
    target = home[:, :, 0]
    earlier = jnp.arange(local)[:, None] > jnp.arange(local)[None, :]
    same = target[:, :, None] == target[:, None, :]
    rank = jnp.sum((same & earlier[None]).astype(jnp.int32), axis=2)
    slot = (jnp.arange(groups, dtype=jnp.int32)[:, None] * owners + target) * slots + rank
    near = neighbours.reshape(local, -1)

    def exchange(array):
        return lax.all_to_all(array, ("grp", "orient"), split_axis=0, concat_axis=0, tiled=True)

    sent = [pack(c, shifts, slot, images, ctf, near, devices, slots) for c in range(CHUNKS)]
    arrived = exchange(sent[0])
    tables = tabulate(references[0], sent[0])
    last, tables = lax.optimization_barrier((sent[1], tables))
    arrived_last = exchange(last)
    score = match(0, arrived, noise_weight, tables)
    scored = match(1, arrived_last, noise_weight, tables, score)
    returned = exchange(scored).reshape(total, -1)
    chosen = (
        slot.T.reshape(-1)[:, None] == jnp.arange(total, dtype=jnp.int32)[None, :]
    ).astype(jnp.float32)
    return jnp.dot(chosen, returned, precision=lax.Precision.HIGHEST).reshape(local, groups, -1)


def solution(mesh):
    in_specs = (
        P(("grp", "orient"), None, None),
        P(("grp", "orient"), None),
        P(("grp", "orient"), None),
        P(None, ("grp", "orient"), None),
        P(("grp", "orient"), None, None),
        P("grp", "orient", None, None),
        P("grp", None),
    )
    out_specs = P(("grp", "orient"), None, None)
    return jax.shard_map(
        per_device, mesh=mesh, in_specs=in_specs, out_specs=out_specs, check_vma=False
    )
```

time: 239 us -> 221 us (0.925)
  local copies, waits for them, and re-layouts: 49 us -> 4.56 us
  other arithmetic: 33.3 us -> 1.74 us
  Pallas kernels: 46.2 us -> 72.6 us
  waiting for transfers between devices: 77.5 us -> 101 us
  blocking collectives: 0 us -> 19.4 us
  starting transfers between devices: 30.9 us -> 21.2 us
    slice x2 -> x0, local copies, waits for them, and re-layouts: 43 us -> none  [the longest x1 37.6 us: per_device(): ref_real, ref_imag = (references[0, :, 0], references[0, :, 1])]
    convert_element_type x2 -> x0, other arithmetic: 31.5 us -> none  [the longest x1 31.5 us: per_device(): (wide_real * wide_real + wide_imag * wide_imag).astype(jnp.bfloat16)]
    pallas_call x5, Pallas kernels: 46.2 us -> 72.6 us  [the longest x1 31.3 us: tabulate(): pl.pallas_call(table_kernel, grid=(orients // rows,), in_specs=[pl.BlockS...]
    all_to_all x3 -> x2, waiting for transfers between devices: 77.5 us -> 101 us  [exchange(): lax.all_to_all(array, ('grp', 'orient'), split_axis=0, concat_axis=0, til...]
    all_to_all x0 -> x1, blocking collectives: none -> 19.4 us  [exchange(): lax.all_to_all(array, ('grp', 'orient'), split_axis=0, concat_axis=0, til...]
    all_to_all x3 -> x2, starting transfers between devices: 30.9 us -> 21.2 us  [exchange(): lax.all_to_all(array, ('grp', 'orient'), split_axis=0, concat_axis=0, til...]
  transfers between devices with their start and end apart: 3 -> 2, of which waited for: 2 -> 2; matrix products, arithmetic and copies ran while one was open for 29% -> 0% of each run, Pallas kernels for 9% -> 23%
where the time goes in v2:
time: 221 us
  waiting for transfers between devices  101 us (46%)
  Pallas kernels  72.6 us (33%)
  starting transfers between devices  21.2 us (10%)
  blocking collectives  19.4 us (9%)
  local copies, waits for them, and re-layouts  4.56 us (2%)
    all_to_all x2, waiting for transfers between devices, exchange(): lax.all_to_all(array, ('grp', 'orient'), split_axis=0, concat_axis=0, til...  101 us
    pallas_call x1, Pallas kernels, tabulate(): pl.pallas_call(table_kernel, grid=(orients // rows,), in_specs=[pl.BlockS...  31.3 us
    all_to_all x2, starting transfers between devices, exchange(): lax.all_to_all(array, ('grp', 'orient'), split_axis=0, concat_axis=0, til...  21.2 us
    all_to_all x1, blocking collectives, exchange(): lax.all_to_all(array, ('grp', 'orient'), split_axis=0, concat_axis=0, til...  19.4 us
    pallas_call x2, Pallas kernels, pack(): pl.pallas_call(body, grid=(1,), in_specs=[whole(shifts), whole(slot), pl....  18.9 us
    pallas_call x1, Pallas kernels, match(): pl.pallas_call(match_last, in_specs=in_specs + [full, extra], out_specs=p...  11.5 us
    pallas_call x1, Pallas kernels, match(): pl.pallas_call(match_first, in_specs=in_specs, out_specs=full, out_shape=...  10.8 us
  transfers between devices with their start and end apart: 2, of which 2 were waited for; matrix products, arithmetic and copies ran while one was open for 0% of the time, Pallas kernels for 23%

profile of v2, /device:TPU:1, one launch (start us, length us, event | category | flops | bytes accessed | tf_op | source)
XLA Modules:
  0.0 220.8 jit_solution(13142694891392366797)
XLA Ops:
  0.0 0.8 copy.11.refs_0_
  0.8 0.8 copy.16
  1.6 1.0 convert_reduce_fusion
  2.6 0.8 multiply_add_fusion.refs_1_
  3.4 0.0 copy-start
  3.4 1.2 copy-done
  4.6 0.0 copy-start.2
  4.6 1.0 copy-done.2
  5.6 0.0 copy-start.1
  5.6 0.0 copy-start.3
  5.6 9.7 %pack_0.1.after_ref = bf16[128,96,2,128]{3,2,1,0:T(2,128)(2,1)} custom-call(s32[32,2]{1,0:T(8,128)S(1)} %copy.11.refs_0_, s32[4,32]{1,0:T(4,128)S(1)} %multiply_add_fusion.refs_1_, bf16[32,2,8192]{2,1,0:T(2,128)(2,1)S(1)} %copy-done, bf16[32,8192]{1,0:T(8,128)(2,1)S(1)} %copy-done.2, s32[32,512]{1,0:T(8,128)S(1)} %bitcast.14), custom_call_target="tpu_custom_call" | custom-call | flops 201326592 | bytes 7077888 | tf_op jit(solution)/shard_map/pack_0/pallas_call | solution.py:99
  15.3 11.9 %all-to-all-start.1 = ((bf16[128,96,2,128]{3,2,1,0:T(2,128)(2,1)}), bf16[128,96,2,128]{3,2,1,0:T(2,128)(2,1)}, u32[]{:S(2)}, u32[]{:S(2)}) async-start(bf16[128,96,2,128]{3,2,1,0:T(2,128)(2,1)} %pack_0.1.after_ref), calls=%async_computation.1 | async-start | bytes 12582912 | tf_op jit(solution)/shard_map/all_to_all | solution.py:277
  27.2 0.0 copy-done.1
  27.2 0.0 copy-done.3
  27.3 9.2 %pack_1.1 = bf16[128,98,2,128]{3,2,1,0:T(2,128)(2,1)} custom-call(s32[32,2]{1,0:T(8,128)S(1)} %copy.11.refs_0_, s32[4,32]{1,0:T(4,128)S(1)} %multiply_add_fusion.refs_1_, bf16[32,2,8192]{2,1,0:T(2,128)(2,1)S(1)} %copy-done.1, bf16[32,8192]{1,0:T(8,128)(2,1)S(1)} %copy-done.3, s32[32,512]{1,0:T(8,128)S(1)} %bitcast.15), custom_call_target="tpu_custom_call" | custom-call | flops 205520896 | bytes 7225344 | tf_op jit(solution)/shard_map/pack_1/pallas_call | solution.py:99
  36.5 31.3 %tabulate.1 = (bf16[512,8192]{1,0:T(8,128)(2,1)}, bf16[512,8192]{1,0:T(8,128)(2,1)}, bf16[512,8192]{1,0:T(8,128)(2,1)}) custom-call(bf16[512,2,8192]{2,1,0:T(2,128)(2,1)} %bitcast.21, bf16[128,96,2,128]{3,2,1,0:T(2,128)(2,1)} %pack_0.1.after_ref), custom_call_target="tpu_custom_call" | custom-call | flops 8589934592 | bytes 41943040 | tf_op jit(solution)/shard_map/tabulate/pallas_call | solution.py:142
  67.8 0.0 copy-start.4
  67.8 34.9 %all-to-all-done.1.arrived_ref = bf16[128,96,2,128]{3,2,1,0:T(2,128)(2,1)} async-done(((bf16[128,96,2,128]{3,2,1,0:T(2,128)(2,1)}), bf16[128,96,2,128]{3,2,1,0:T(2,128)(2,1)}, u32[]{:S(2)}, u32[]{:S(2)}) %all-to-all-start.1) | async-done | bytes 6291488 | tf_op jit(solution)/shard_map/all_to_all | solution.py:277
  102.7 9.3 %all-to-all-start = ((bf16[128,98,2,128]{3,2,1,0:T(2,128)(2,1)}), bf16[128,98,2,128]{3,2,1,0:T(2,128)(2,1)}, u32[]{:S(2)}, u32[]{:S(2)}) async-start(bf16[128,98,2,128]{3,2,1,0:T(2,128)(2,1)} %pack_1.1), calls=%async_computation | async-start | bytes 12845056 | tf_op jit(solution)/shard_map/all_to_all | solution.py:277
  111.9 0.0 copy-done.4
  112.0 10.8 %match_0.1.base_ref = f32[256,512]{1,0:T(8,128)S(1)} custom-call(bf16[128,96,2,128]{3,2,1,0:T(2,128)(2,1)} %all-to-all-done.1.arrived_ref, f32[1,8192]{1,0:T(1,128)S(1)} %copy-done.4, bf16[512,8192]{1,0:T(8,128)(2,1)} %get-tuple-element.16.re_ref, bf16[512,8192]{1,0:T(8,128)(2,1)} %get-tuple-element.17.im_ref, bf16[512,8192]{1,0:T(8,128)(2,1)} %get-tuple-element.18.pw_ref), custom_call_target="tpu_custom_call" | custom-call | flops 3221225472 | bytes 18874368 | tf_op jit(solution)/shard_map/match_0/pallas_call | solution.py:244
  122.8 66.2 %all-to-all-done.arrived_ref.near_ref = bf16[128,98,2,128]{3,2,1,0:T(2,128)(2,1)} async-done(((bf16[128,98,2,128]{3,2,1,0:T(2,128)(2,1)}), bf16[128,98,2,128]{3,2,1,0:T(2,128)(2,1)}, u32[]{:S(2)}, u32[]{:S(2)}) %all-to-all-start) | async-done | bytes 6422560 | tf_op jit(solution)/shard_map/all_to_all | solution.py:277
  188.9 11.5 %match_1.1 = f32[128,2,128]{2,1,0:T(2,128)S(1)} custom-call(bf16[128,98,2,128]{3,2,1,0:T(2,128)(2,1)} %all-to-all-done.arrived_ref.near_ref, f32[1,8192]{1,0:T(1,128)S(1)} %copy-done.4, bf16[512,8192]{1,0:T(8,128)(2,1)} %get-tuple-element.16.re_ref, bf16[512,8192]{1,0:T(8,128)(2,1)} %get-tuple-element.17.im_ref, bf16[512,8192]{1,0:T(8,128)(2,1)} %get-tuple-element.18.pw_ref, ...), custom_call_target="tpu_custom_call" | custom-call | flops 3288334336 | bytes 19267584 | tf_op jit(solution)/shard_map/match_1/pallas_call | solution.py:252
  200.4 19.4 %all_to_all.15 = f32[128,2,128]{2,1,0:T(2,128)S(1)} all-to-all(f32[128,2,128]{2,1,0:T(2,128)S(1)} %match_1.1), channel_id=1, replica_groups=mesh['grp'=4,'orient'=32] {'grp','orient'}, dimensions={0} | all-to-all | bytes 262144 | tf_op jit(solution)/shard_map/all_to_all | solution.py:277
  219.9 0.3 fusion.1
  220.1 0.7 copy.13
  (2 shorter events, 0.0 us)
Async XLA Ops:
  3.4 1.2 copy-start
  4.6 1.0 copy-start.2
  5.6 21.6 %copy-start.1 = (bf16[32,2,8192]{2,1,0:T(2,128)(2,1)S(1)}, bf16[32,2,8192]{2,1,0:T(2,128)(2,1)}, u32[]{:S(2)}) copy-start(bf16[32,2,8192]{2,1,0:T(2,128)(2,1)} %refs_2_.3) | copy-start | bytes 3145732
  5.6 21.6 %copy-start.3 = (bf16[32,8192]{1,0:T(8,128)(2,1)S(1)}, bf16[32,8192]{1,0:T(8,128)(2,1)}, u32[]{:S(2)}) copy-start(bf16[32,8192]{1,0:T(8,128)(2,1)} %refs_3_.3) | copy-start | bytes 1572868
  15.3 87.3 %all-to-all-start.1 = ((bf16[128,96,2,128]{3,2,1,0:T(2,128)(2,1)}), bf16[128,96,2,128]{3,2,1,0:T(2,128)(2,1)}, u32[]{:S(2)}, u32[]{:S(2)}) async-start(bf16[128,96,2,128]{3,2,1,0:T(2,128)(2,1)} %pack_0.1.after_ref), calls=%async_computation.1 | async-start | bytes 12582912 | tf_op jit(solution)/shard_map/all_to_all | solution.py:277
  67.8 44.1 %copy-start.4 = (f32[1,8192]{1,0:T(1,128)S(1)}, f32[1,8192]{1,0:T(1,128)}, u32[]{:S(2)}) copy-start(f32[1,8192]{1,0:T(1,128)} %weight_ref.3) | copy-start | bytes 98308
  102.7 86.3 %all-to-all-start = ((bf16[128,98,2,128]{3,2,1,0:T(2,128)(2,1)}), bf16[128,98,2,128]{3,2,1,0:T(2,128)(2,1)}, u32[]{:S(2)}, u32[]{:S(2)}) async-start(bf16[128,98,2,128]{3,2,1,0:T(2,128)(2,1)} %pack_1.1), calls=%async_computation | async-start | bytes 12845056 | tf_op jit(solution)/shard_map/all_to_all | solution.py:277

commit v3 on v2

--- a/solution.py
+++ b/solution.py
@@ -35,63 +35,94 @@
     )
 
 
-def pack_kernel(chunk, width, shift_ref, slot_ref, image_ref, ctf_ref, near_ref, out_ref, pair_ref):
+def pack_kernel(chunk, width, shift_ref, home_ref, image_ref, ctf_ref, *refs):
+    *near_refs, out_ref, held, pair, sems = refs
     local = shift_ref.shape[0]
-    groups = slot_ref.shape[0]
+    groups = home_ref.shape[0]
     devices, depth, slots, _ = out_ref.shape
-    total = devices * slots
+    share = devices // groups
+    step_planes = 3 * GROUP
     move_x = jnp.broadcast_to(shift_ref[:, 0:1].astype(jnp.float32), (local, LANES))
     move_y = jnp.broadcast_to(shift_ref[:, 1:2].astype(jnp.float32), (local, LANES))
-    place = lax.broadcasted_iota(jnp.int32, (total, local), 0)
-    hit = place == slot_ref[0:1, :]
-    for g in range(1, groups):
-        hit = hit | (place == slot_ref[g : g + 1, :])
-    select = jnp.where(hit, 1.0, 0.0).astype(jnp.bfloat16)
-
-    def spread(rows, payload):
-        return jnp.dot(rows, payload, preferred_element_type=jnp.float32).astype(jnp.bfloat16)
-
-    def one(r, carry):
-        cols = pl.ds(pl.multiple_of(r * LANES, LANES), LANES)
-        cosine, sine = rotation(move_x, move_y, chunk * width + r)
-        pair_ref[...] = image_ref[:, :, cols].reshape(2 * local, LANES).astype(jnp.float32)
-        real = pair_ref[pl.ds(0, local, stride=2), :]
-        imag = pair_ref[pl.ds(1, local, stride=2), :]
-        payload = jnp.concatenate(
-            [
-                (real * cosine + imag * sine).astype(jnp.bfloat16),
-                (imag * cosine - real * sine).astype(jnp.bfloat16),
-                ctf_ref[:, cols],
-            ],
-            axis=1,
-        )
-        packed = spread(select, payload)
-        for part in range(3):
-            piece = packed[:, part * LANES : (part + 1) * LANES]
-            out_ref[:, 3 * r + part] = piece.reshape(devices, slots, LANES)
+    row = lax.broadcasted_iota(jnp.int32, (share * slots, local), 0)
+    hit = jnp.concatenate(
+        [
+            jnp.where(row // slots == home_ref[g : g + 1, :], 1.0, 0.0)
+            for g in range(groups)
+        ],
+        axis=0,
+    )
+    before = lax.broadcasted_iota(jnp.int32, (local, local), 0)
+    after = lax.broadcasted_iota(jnp.int32, (local, local), 1)
+    earlier = jnp.where(before < after, 1.0, 0.0).astype(jnp.bfloat16)
+    rank = jnp.dot(hit.astype(jnp.bfloat16), earlier, preferred_element_type=jnp.float32)
+    row = lax.broadcasted_iota(jnp.int32, hit.shape, 0)
+    mine = rank == (row % slots).astype(jnp.float32)
+    select = jnp.where(mine, hit, 0.0).astype(jnp.bfloat16)
+
+    def send(i):
+        planes = pl.ds(i * step_planes, step_planes)
+        return pltpu.make_async_copy(held.at[:, planes], out_ref.at[:, planes], sems.at[i])
+
+    def one(i, carry):
+        sides = ([], [], [])
+        for r in range(GROUP):
+            at = i * GROUP + r
+            cols = pl.ds(pl.multiple_of(at * LANES, LANES), LANES)
+            cosine, sine = rotation(move_x, move_y, chunk * width + at)
+            pair[r] = image_ref[:, :, cols].reshape(2 * local, LANES).astype(jnp.float32)
+            real = pair[r, pl.ds(0, local, stride=2), :]
+            imag = pair[r, pl.ds(1, local, stride=2), :]
+            sides[0].append((real * cosine + imag * sine).astype(jnp.bfloat16))
+            sides[1].append((imag * cosine - real * sine).astype(jnp.bfloat16))
+            sides[2].append(ctf_ref[:, cols])
+        for r in range(0, GROUP, 2):
+            payload = jnp.concatenate([side[r + k] for k in range(2) for side in sides], axis=1)
+            packed = jnp.dot(select, payload, preferred_element_type=jnp.float32).astype(
+                jnp.bfloat16
+            )
+            for k in range(2):
+                for part in range(3):
+                    column = (3 * k + part) * LANES
+                    held[:, i * step_planes + part * GROUP + r + k] = packed[
+                        :, column : column + LANES
+                    ].reshape(devices, slots, LANES)
+        send(i).start()
         return carry
 
-    lax.fori_loop(0, width, one, 0, unroll=2)
-    if depth > 3 * width:
-        share = total // groups
+    steps = width // GROUP
+    lax.fori_loop(0, steps, one, 0)
+    if near_refs:
         halves = ([], [])
         for g in range(groups):
-            near = near_ref[:, g * NEAR : (g + 1) * NEAR]
+            chosen = select[g * share * slots : (g + 1) * share * slots]
+            near = near_refs[0][:, g * NEAR : (g + 1) * NEAR]
             for half, value in zip(halves, (near >> 1, near & 1)):
                 half.append(
-                    spread(select[g * share : (g + 1) * share], value.astype(jnp.float32).astype(jnp.bfloat16))
+                    jnp.dot(
+                        chosen,
+                        value.astype(jnp.float32).astype(jnp.bfloat16),
+                        preferred_element_type=jnp.float32,
+                    ).astype(jnp.bfloat16)
                 )
         for at, half in enumerate(halves):
-            out_ref[:, 3 * width + at] = jnp.concatenate(half, axis=0).reshape(devices, slots, NEAR)
-
-
-def pack(chunk, shifts, slot, images, ctf, near, devices, slots):
+            held[:, 3 * width + at] = jnp.concatenate(half, axis=0).reshape(devices, slots, NEAR)
+        tail = pl.ds(3 * width, 2)
+        rest = pltpu.make_async_copy(held.at[:, tail], out_ref.at[:, tail], sems.at[steps])
+        rest.start()
+        rest.wait()
+    for i in range(steps):
+        send(i).wait()
+
+
+def pack(chunk, shifts, home, images, ctf, near, devices, slots):
     local = shifts.shape[0]
     width = SLABS // CHUNKS
     span = width * LANES
-    depth = 3 * width + (2 if chunk == CHUNKS - 1 else 0)
+    extra = 2 if chunk == CHUNKS - 1 else 0
+    shape = (devices, 3 * width + extra, slots, LANES)
+    more = (near,) if extra else ()
     whole = lambda array: pl.BlockSpec(array.shape, lambda i: (0, 0))
-    shape = (devices, depth, slots, LANES)
 
     def body(*refs):
         pack_kernel(chunk, width, *refs)
@@ -101,22 +132,26 @@
         grid=(1,),
         in_specs=[
             whole(shifts),
-            whole(slot),
+            whole(home),
             pl.BlockSpec((local, 2, span), lambda i: (0, 0, chunk)),
             pl.BlockSpec((local, span), lambda i: (0, chunk)),
-            whole(near),
+            *(whole(array) for array in more),
         ],
-        out_specs=pl.BlockSpec(shape, lambda i: (0, 0, 0, 0)),
+        out_specs=pl.BlockSpec(memory_space=pl.ANY),
         out_shape=jax.ShapeDtypeStruct(shape, jnp.bfloat16),
-        scratch_shapes=[pltpu.VMEM((2 * local, LANES), jnp.float32)],
+        scratch_shapes=[
+            pltpu.VMEM(shape, jnp.bfloat16),
+            pltpu.VMEM((GROUP, 2 * local, LANES), jnp.float32),
+            pltpu.SemaphoreType.DMA((width // GROUP + 1,)),
+        ],
         cost_estimate=pl.CostEstimate(
-            flops=2 * devices * slots * local * depth * LANES,
-            bytes_accessed=2 * depth * LANES * (devices * slots + local),
+            flops=2 * devices * slots * local * shape[1] * LANES,
+            bytes_accessed=2 * shape[1] * LANES * (devices * slots + local),
             transcendentals=0,
         ),
-        compiler_params=pltpu.CompilerParams(vmem_limit_bytes=48 * 2**20),
+        compiler_params=pltpu.CompilerParams(vmem_limit_bytes=63 * 2**20),
         name=f"pack_{chunk}",
-    )(shifts, slot, images, ctf, near)
+    )(shifts, home, images, ctf, *more)
 
 
 def table_kernel(block_ref, after_ref, re_ref, im_ref, pw_ref, pair_ref):
@@ -161,7 +196,7 @@
     sides = ([], [], [])
     for r in range(GROUP):
         real, imag, ctf = (
-            arrived_ref[:, 3 * r + part].reshape(rows, LANES).astype(jnp.float32)
+            arrived_ref[:, part * GROUP + r].reshape(rows, LANES).astype(jnp.float32)
             for part in range(3)
         )
         tone = ctf * weight_ref[:, r * LANES : (r + 1) * LANES]
@@ -276,7 +311,7 @@
     def exchange(array):
         return lax.all_to_all(array, ("grp", "orient"), split_axis=0, concat_axis=0, tiled=True)
 
-    sent = [pack(c, shifts, slot, images, ctf, near, devices, slots) for c in range(CHUNKS)]
+    sent = [pack(c, shifts, target, images, ctf, near, devices, slots) for c in range(CHUNKS)]
     arrived = exchange(sent[0])
     tables = tabulate(references[0], sent[0])
     last, tables = lax.optimization_barrier((sent[1], tables))

time: 221 us -> 216 us (0.977)
  blocking collectives: 19.4 us -> 0 us
  waiting for transfers between devices: 101 us -> 111 us
  starting transfers between devices: 21.2 us -> 30.8 us
  Pallas kernels: 72.6 us -> 70.3 us
    all_to_all x1 -> x0, blocking collectives: 19.4 us -> none  [exchange(): lax.all_to_all(array, ('grp', 'orient'), split_axis=0, concat_axis=0, til...]
    all_to_all x2 -> x3, waiting for transfers between devices: 101 us -> 111 us  [exchange(): lax.all_to_all(array, ('grp', 'orient'), split_axis=0, concat_axis=0, til...]
    all_to_all x2 -> x3, starting transfers between devices: 21.2 us -> 30.8 us  [exchange(): lax.all_to_all(array, ('grp', 'orient'), split_axis=0, concat_axis=0, til...]
    pallas_call x2, Pallas kernels: 18.9 us -> 16.3 us  [pack(): pl.pallas_call(body, grid=(1,), in_specs=[whole(shifts), whole(home), pl....]
  transfers between devices with their start and end apart: 2 -> 3, of which waited for: 2 -> 3; matrix products, arithmetic and copies ran while one was open for 0% -> 0% of each run, Pallas kernels for 23% -> 23%
where the time goes in v3:
time: 216 us; the launch traced here: 215 us
  waiting for transfers between devices  111 us (51%)
  Pallas kernels  70.3 us (33%)
  starting transfers between devices  30.8 us (14%)
  local copies, waits for them, and re-layouts  2.68 us (1%)
    all_to_all x3, waiting for transfers between devices, exchange(): lax.all_to_all(array, ('grp', 'orient'), split_axis=0, concat_axis=0, til...  111 us
    pallas_call x1, Pallas kernels, tabulate(): pl.pallas_call(table_kernel, grid=(orients // rows,), in_specs=[pl.BlockS...  31 us
    all_to_all x3, starting transfers between devices, exchange(): lax.all_to_all(array, ('grp', 'orient'), split_axis=0, concat_axis=0, til...  30.8 us
    pallas_call x2, Pallas kernels, pack(): pl.pallas_call(body, grid=(1,), in_specs=[whole(shifts), whole(home), pl....  16.3 us
    pallas_call x1, Pallas kernels, match(): pl.pallas_call(match_last, in_specs=in_specs + [full, extra], out_specs=p...  12.1 us
    pallas_call x1, Pallas kernels, match(): pl.pallas_call(match_first, in_specs=in_specs, out_specs=full, out_shape=...  10.8 us
  transfers between devices with their start and end apart: 3, of which 3 were waited for; matrix products, arithmetic and copies ran while one was open for 0% of the time, Pallas kernels for 23%

profile of v3, /device:TPU:1, one launch (start us, length us, event | category | flops | bytes accessed | tf_op | source)
XLA Modules:
  0.0 215.5 jit_solution(11478227806669884041)
XLA Ops:
  0.0 1.4 copy.11.refs_0_
  1.4 0.0 copy-start.1
  1.4 8.1 %pack_0.1.after_ref = bf16[128,96,2,128]{3,2,1,0:T(2,128)(2,1)} custom-call(s32[32,2]{1,0:T(8,128)} %copy.11.refs_0_, s32[4,32]{1,0:T(4,128)} %bitcast.18, bf16[32,2,8192]{2,1,0:T(2,128)(2,1)} %refs_2_.3, bf16[32,8192]{1,0:T(8,128)(2,1)} %refs_3_.3), custom_call_target="tpu_custom_call" | custom-call | flops 201326592 | bytes 7077888 | tf_op jit(solution)/shard_map/pack_0/pallas_call | solution.py:130
  9.4 11.9 %all-to-all-start.1 = ((bf16[128,96,2,128]{3,2,1,0:T(2,128)(2,1)}), bf16[128,96,2,128]{3,2,1,0:T(2,128)(2,1)}, u32[]{:S(2)}, u32[]{:S(2)}) async-start(bf16[128,96,2,128]{3,2,1,0:T(2,128)(2,1)} %pack_0.1.after_ref), calls=%async_computation.1 | async-start | bytes 12582912 | tf_op jit(solution)/shard_map/all_to_all | solution.py:312
  21.3 0.0 copy-done.1
  21.3 0.6 copy.16
  22.0 8.3 %pack_1.1 = bf16[128,98,2,128]{3,2,1,0:T(2,128)(2,1)} custom-call(s32[32,2]{1,0:T(8,128)} %copy.11.refs_0_, s32[4,32]{1,0:T(4,128)} %bitcast.19, bf16[32,2,8192]{2,1,0:T(2,128)(2,1)} %refs_2_.3, bf16[32,8192]{1,0:T(8,128)(2,1)} %refs_3_.3, s32[32,512]{1,0:T(8,128)} %bitcast.16), custom_call_target="tpu_custom_call" | custom-call | flops 205520896 | bytes 7225344 | tf_op jit(solution)/shard_map/pack_1/pallas_call | solution.py:130
  30.2 31.0 %tabulate.1 = (bf16[512,8192]{1,0:T(8,128)(2,1)}, bf16[512,8192]{1,0:T(8,128)(2,1)}, bf16[512,8192]{1,0:T(8,128)(2,1)}) custom-call(bf16[512,2,8192]{2,1,0:T(2,128)(2,1)} %bitcast.22, bf16[128,96,2,128]{3,2,1,0:T(2,128)(2,1)} %pack_0.1.after_ref), custom_call_target="tpu_custom_call" | custom-call | flops 8589934592 | bytes 41943040 | tf_op jit(solution)/shard_map/tabulate/pallas_call | solution.py:177
  61.3 0.0 copy-start.2
  61.3 0.0 copy-start
  61.3 35.5 %all-to-all-done.1.arrived_ref = bf16[128,96,2,128]{3,2,1,0:T(2,128)(2,1)} async-done(((bf16[128,96,2,128]{3,2,1,0:T(2,128)(2,1)}), bf16[128,96,2,128]{3,2,1,0:T(2,128)(2,1)}, u32[]{:S(2)}, u32[]{:S(2)}) %all-to-all-start.1) | async-done | bytes 6291488 | tf_op jit(solution)/shard_map/all_to_all | solution.py:312
  96.8 9.3 %all-to-all-start = ((bf16[128,98,2,128]{3,2,1,0:T(2,128)(2,1)}), bf16[128,98,2,128]{3,2,1,0:T(2,128)(2,1)}, u32[]{:S(2)}, u32[]{:S(2)}) async-start(bf16[128,98,2,128]{3,2,1,0:T(2,128)(2,1)} %pack_1.1), calls=%async_computation | async-start | bytes 12845056 | tf_op jit(solution)/shard_map/all_to_all | solution.py:312
  106.1 0.0 copy-done.2
  106.1 0.2 convert_reduce_fusion
  106.3 0.0 copy-done
  106.3 10.8 %match_0.1.base_ref = f32[256,512]{1,0:T(8,128)S(1)} custom-call(bf16[128,96,2,128]{3,2,1,0:T(2,128)(2,1)} %all-to-all-done.1.arrived_ref, f32[1,8192]{1,0:T(1,128)S(1)} %copy-done, bf16[512,8192]{1,0:T(8,128)(2,1)} %get-tuple-element.16.re_ref, bf16[512,8192]{1,0:T(8,128)(2,1)} %get-tuple-element.17.im_ref, bf16[512,8192]{1,0:T(8,128)(2,1)} %get-tuple-element.18.pw_ref), custom_call_target="tpu_custom_call" | custom-call | flops 3221225472 | bytes 18874368 | tf_op jit(solution)/shard_map/match_0/pallas_call | solution.py:279
  117.1 65.9 %all-to-all-done.arrived_ref.near_ref = bf16[128,98,2,128]{3,2,1,0:T(2,128)(2,1)} async-done(((bf16[128,98,2,128]{3,2,1,0:T(2,128)(2,1)}), bf16[128,98,2,128]{3,2,1,0:T(2,128)(2,1)}, u32[]{:S(2)}, u32[]{:S(2)}) %all-to-all-start) | async-done | bytes 6422560 | tf_op jit(solution)/shard_map/all_to_all | solution.py:312
  183.0 12.1 %match_1.1 = f32[128,2,128]{2,1,0:T(2,128)} custom-call(bf16[128,98,2,128]{3,2,1,0:T(2,128)(2,1)} %all-to-all-done.arrived_ref.near_ref, f32[1,8192]{1,0:T(1,128)S(1)} %copy-done, bf16[512,8192]{1,0:T(8,128)(2,1)} %get-tuple-element.16.re_ref, bf16[512,8192]{1,0:T(8,128)(2,1)} %get-tuple-element.17.im_ref, bf16[512,8192]{1,0:T(8,128)(2,1)} %get-tuple-element.18.pw_ref, ...), custom_call_target="tpu_custom_call" | custom-call | flops 3288334336 | bytes 19267584 | tf_op jit(solution)/shard_map/match_1/pallas_call | solution.py:287
  195.1 9.6 %all-to-all-start.2 = ((f32[128,2,128]{2,1,0:T(2,128)}), f32[128,2,128]{2,1,0:T(2,128)S(1)}, u32[]{:S(2)}, u32[]{:S(2)}) async-start(f32[128,2,128]{2,1,0:T(2,128)} %match_1.1), calls=%async_computation.2 | async-start | bytes 262144 | tf_op jit(solution)/shard_map/all_to_all | solution.py:312
  204.8 0.1 add_bitcast_fusion
  204.9 9.7 %all-to-all-done.2 = f32[128,2,128]{2,1,0:T(2,128)S(1)} async-done(((f32[128,2,128]{2,1,0:T(2,128)}), f32[128,2,128]{2,1,0:T(2,128)S(1)}, u32[]{:S(2)}, u32[]{:S(2)}) %all-to-all-start.2) | async-done | bytes 131104 | tf_op jit(solution)/shard_map/all_to_all | solution.py:312
  214.5 0.3 fusion.1
  214.8 0.7 copy.13
  (2 shorter events, 0.0 us)
Async XLA Ops:
  1.4 20.0 %copy-start.1 = (s32[32,4,128]{2,1,0:T(4,128)S(1)}, s32[32,4,128]{2,1,0:T(4,128)}, u32[]{:S(2)}) copy-start(s32[32,4,128]{2,1,0:T(4,128)} %param.11) | copy-start | bytes 196612
  9.4 87.3 %all-to-all-start.1 = ((bf16[128,96,2,128]{3,2,1,0:T(2,128)(2,1)}), bf16[128,96,2,128]{3,2,1,0:T(2,128)(2,1)}, u32[]{:S(2)}, u32[]{:S(2)}) async-start(bf16[128,96,2,128]{3,2,1,0:T(2,128)(2,1)} %pack_0.1.after_ref), calls=%async_computation.1 | async-start | bytes 12582912 | tf_op jit(solution)/shard_map/all_to_all | solution.py:312
  61.3 44.8 %copy-start.2 = (s32[4,32,1]{1,2,0:T(1,128)S(1)}, s32[4,32,1]{1,2,0:T(1,128)}, u32[]{:S(2)}) copy-start(s32[4,32,1]{1,2,0:T(1,128)} %param.10) | copy-start | bytes 1540
  61.3 45.0 %copy-start = (f32[1,8192]{1,0:T(1,128)S(1)}, f32[1,8192]{1,0:T(1,128)}, u32[]{:S(2)}) copy-start(f32[1,8192]{1,0:T(1,128)} %weight_ref.3) | copy-start | bytes 98308
  96.8 86.3 %all-to-all-start = ((bf16[128,98,2,128]{3,2,1,0:T(2,128)(2,1)}), bf16[128,98,2,128]{3,2,1,0:T(2,128)(2,1)}, u32[]{:S(2)}, u32[]{:S(2)}) async-start(bf16[128,98,2,128]{3,2,1,0:T(2,128)(2,1)} %pack_1.1), calls=%async_computation | async-start | bytes 12845056 | tf_op jit(solution)/shard_map/all_to_all | solution.py:312
  195.1 19.4 %all-to-all-start.2 = ((f32[128,2,128]{2,1,0:T(2,128)}), f32[128,2,128]{2,1,0:T(2,128)S(1)}, u32[]{:S(2)}, u32[]{:S(2)}) async-start(f32[128,2,128]{2,1,0:T(2,128)} %match_1.1), calls=%async_computation.2 | async-start | bytes 262144 | tf_op jit(solution)/shard_map/all_to_all | solution.py:312

commit v4 on v3

--- a/solution.py
+++ b/solution.py
@@ -11,7 +11,7 @@
 PIX = 8192
 LANES = 128
 SLABS = PIX // LANES
-CHUNKS = 2
+WIDTHS = (48, 16)
 GROUP = 8
 NEAR = 128
 
@@ -35,15 +35,26 @@
     )
 
 
-def pack_kernel(chunk, width, shift_ref, home_ref, image_ref, ctf_ref, *refs):
+def pack_kernel(first, width, shift_ref, home_ref, image_ref, ctf_ref, *refs):
     *near_refs, out_ref, held, pair, sems = refs
-    local = shift_ref.shape[0]
+    local = shift_ref.shape[1]
     groups = home_ref.shape[0]
     devices, depth, slots, _ = out_ref.shape
     share = devices // groups
     step_planes = 3 * GROUP
-    move_x = jnp.broadcast_to(shift_ref[:, 0:1].astype(jnp.float32), (local, LANES))
-    move_y = jnp.broadcast_to(shift_ref[:, 1:2].astype(jnp.float32), (local, LANES))
+    before = lax.broadcasted_iota(jnp.int32, (local, local), 0)
+    after = lax.broadcasted_iota(jnp.int32, (local, local), 1)
+    move_x, move_y = (
+        jnp.broadcast_to(
+            jnp.sum(
+                jnp.where(before == after, shift_ref[axis : axis + 1, :].astype(jnp.float32), 0.0),
+                axis=1,
+                keepdims=True,
+            ),
+            (local, LANES),
+        )
+        for axis in range(2)
+    )
     row = lax.broadcasted_iota(jnp.int32, (share * slots, local), 0)
     hit = jnp.concatenate(
         [
@@ -52,8 +63,6 @@
         ],
         axis=0,
     )
-    before = lax.broadcasted_iota(jnp.int32, (local, local), 0)
-    after = lax.broadcasted_iota(jnp.int32, (local, local), 1)
     earlier = jnp.where(before < after, 1.0, 0.0).astype(jnp.bfloat16)
     rank = jnp.dot(hit.astype(jnp.bfloat16), earlier, preferred_element_type=jnp.float32)
     row = lax.broadcasted_iota(jnp.int32, hit.shape, 0)
@@ -69,7 +78,7 @@
         for r in range(GROUP):
             at = i * GROUP + r
             cols = pl.ds(pl.multiple_of(at * LANES, LANES), LANES)
-            cosine, sine = rotation(move_x, move_y, chunk * width + at)
+            cosine, sine = rotation(move_x, move_y, first + at)
             pair[r] = image_ref[:, :, cols].reshape(2 * local, LANES).astype(jnp.float32)
             real = pair[r, pl.ds(0, local, stride=2), :]
             imag = pair[r, pl.ds(1, local, stride=2), :]
@@ -117,15 +126,17 @@
 
 def pack(chunk, shifts, home, images, ctf, near, devices, slots):
     local = shifts.shape[0]
-    width = SLABS // CHUNKS
+    shifts = shifts.T
+    width = WIDTHS[chunk]
+    at = sum(WIDTHS[:chunk]) // width
     span = width * LANES
-    extra = 2 if chunk == CHUNKS - 1 else 0
+    extra = 2 if chunk == len(WIDTHS) - 1 else 0
     shape = (devices, 3 * width + extra, slots, LANES)
     more = (near,) if extra else ()
     whole = lambda array: pl.BlockSpec(array.shape, lambda i: (0, 0))
 
     def body(*refs):
-        pack_kernel(chunk, width, *refs)
+        pack_kernel(sum(WIDTHS[:chunk]), width, *refs)
 
     return pl.pallas_call(
         body,
@@ -133,8 +144,8 @@
         in_specs=[
             whole(shifts),
             whole(home),
-            pl.BlockSpec((local, 2, span), lambda i: (0, 0, chunk)),
-            pl.BlockSpec((local, span), lambda i: (0, chunk)),
+            pl.BlockSpec((local, 2, span), lambda i: (0, 0, at)),
+            pl.BlockSpec((local, span), lambda i: (0, at)),
             *(whole(array) for array in more),
         ],
         out_specs=pl.BlockSpec(memory_space=pl.ANY),
@@ -252,15 +263,16 @@
 
 def match(chunk, arrived, weight, tables, base=None):
     devices, depth, slots, _ = arrived.shape
-    width = SLABS // CHUNKS
+    width = WIDTHS[chunk]
     steps = width // GROUP
+    done = sum(WIDTHS[:chunk]) // GROUP
     orients = tables[0].shape[0]
     rows = devices * slots
-    table = pl.BlockSpec((orients, GROUP * LANES), lambda i: (0, chunk * steps + i))
+    table = pl.BlockSpec((orients, GROUP * LANES), lambda i: (0, done + i))
     full = pl.BlockSpec((rows, orients), lambda i: (0, 0))
     in_specs = [
         pl.BlockSpec((devices, 3 * GROUP, slots, LANES), lambda i: (0, i, 0, 0)),
-        pl.BlockSpec((1, GROUP * LANES), lambda i: (0, chunk * steps + i)),
+        pl.BlockSpec((1, GROUP * LANES), lambda i: (0, done + i)),
         table,
         table,
         table,
@@ -272,7 +284,7 @@
             bytes_accessed=2 * depth * LANES * (rows + orients),
             transcendentals=0,
         ),
-        compiler_params=pltpu.CompilerParams(vmem_limit_bytes=48 * 2**20),
+        compiler_params=pltpu.CompilerParams(vmem_limit_bytes=63 * 2**20),
         name=f"match_{chunk}",
     )
     if base is None:
@@ -311,7 +323,7 @@
     def exchange(array):
         return lax.all_to_all(array, ("grp", "orient"), split_axis=0, concat_axis=0, tiled=True)
 
-    sent = [pack(c, shifts, target, images, ctf, near, devices, slots) for c in range(CHUNKS)]
+    sent = [pack(c, shifts, target, images, ctf, near, devices, slots) for c in range(len(WIDTHS))]
     arrived = exchange(sent[0])
     tables = tabulate(references[0], sent[0])
     last, tables = lax.optimization_barrier((sent[1], tables))

time: 216 us -> 218 us (level)
  waiting for transfers between devices: 111 us -> 117 us
  starting transfers between devices: 30.8 us -> 28.1 us
    all_to_all x3, waiting for transfers between devices: 111 us -> 117 us  [exchange(): lax.all_to_all(array, ('grp', 'orient'), split_axis=0, concat_axis=0, til...]
    pallas_call x1, Pallas kernels: 10.8 us -> 16.1 us  [match(): pl.pallas_call(match_first, in_specs=in_specs, out_specs=full, out_shape=...]
    pallas_call x1, Pallas kernels: 12.1 us -> 7.87 us  [match(): pl.pallas_call(match_last, in_specs=in_specs + [full, extra], out_specs=p...]
    all_to_all x3, starting transfers between devices: 30.8 us -> 28.1 us  [exchange(): lax.all_to_all(array, ('grp', 'orient'), split_axis=0, concat_axis=0, til...]
  transfers between devices with their start and end apart: 3 -> 3, of which waited for: 3 -> 3; matrix products, arithmetic and copies ran while one was open for 0% -> 0% of each run, Pallas kernels for 23% -> 24%
where the time goes in v4:
time: 218 us
  waiting for transfers between devices  117 us (54%)
  Pallas kernels  71.1 us (33%)
  starting transfers between devices  28.1 us (13%)
    all_to_all x3, waiting for transfers between devices, exchange(): lax.all_to_all(array, ('grp', 'orient'), split_axis=0, concat_axis=0, til...  117 us
    pallas_call x1, Pallas kernels, tabulate(): pl.pallas_call(table_kernel, grid=(orients // rows,), in_specs=[pl.BlockS...  31 us
    all_to_all x3, starting transfers between devices, exchange(): lax.all_to_all(array, ('grp', 'orient'), split_axis=0, concat_axis=0, til...  28.1 us
    pallas_call x2, Pallas kernels, pack(): pl.pallas_call(body, grid=(1,), in_specs=[whole(shifts), whole(home), pl....  16.2 us
    pallas_call x1, Pallas kernels, match(): pl.pallas_call(match_first, in_specs=in_specs, out_specs=full, out_shape=...  16.1 us
    pallas_call x1, Pallas kernels, match(): pl.pallas_call(match_last, in_specs=in_specs + [full, extra], out_specs=p...  7.87 us
  transfers between devices with their start and end apart: 3, of which 3 were waited for; matrix products, arithmetic and copies ran while one was open for 0% of the time, Pallas kernels for 24%

profile of v4, /device:TPU:1, one launch (start us, length us, event | category | flops | bytes accessed | tf_op | source)
XLA Modules:
  0.0 218.0 jit_solution(13985238521166232625)
XLA Ops:
  0.0 10.9 %pack_0.1.after_ref = bf16[128,144,2,128]{3,2,1,0:T(2,128)(2,1)} custom-call(s32[2,32]{1,0:T(2,128)} %bitcast.23, s32[4,32]{1,0:T(4,128)} %bitcast.19, bf16[32,2,8192]{2,1,0:T(2,128)(2,1)} %refs_2_.3, bf16[32,8192]{1,0:T(8,128)(2,1)} %refs_3_.3), custom_call_target="tpu_custom_call" | custom-call | flops 301989888 | bytes 10616832 | tf_op jit(solution)/shard_map/pack_0/pallas_call | solution.py:141
  10.9 0.0 copy-start
  10.9 11.9 %all-to-all-start.1 = ((bf16[128,144,2,128]{3,2,1,0:T(2,128)(2,1)}), bf16[128,144,2,128]{3,2,1,0:T(2,128)(2,1)}, u32[]{:S(2)}, u32[]{:S(2)}) async-start(bf16[128,144,2,128]{3,2,1,0:T(2,128)(2,1)} %pack_0.1.after_ref), calls=%async_computation.1 | async-start | bytes 18874368 | tf_op jit(solution)/shard_map/all_to_all | solution.py:324
  22.8 0.0 copy-done
  22.8 0.6 copy.12
  23.4 5.3 %pack_1.1 = bf16[128,50,2,128]{3,2,1,0:T(2,128)(2,1)} custom-call(s32[2,32]{1,0:T(2,128)} %bitcast.24, s32[4,32]{1,0:T(4,128)} %bitcast.20, bf16[32,2,8192]{2,1,0:T(2,128)(2,1)} %refs_2_.3, bf16[32,8192]{1,0:T(8,128)(2,1)} %refs_3_.3, s32[32,512]{1,0:T(8,128)} %bitcast.17), custom_call_target="tpu_custom_call" | custom-call | flops 104857600 | bytes 3686400 | tf_op jit(solution)/shard_map/pack_1/pallas_call | solution.py:141
  28.8 0.0 copy-start.1
  28.8 31.0 %tabulate.1 = (bf16[512,8192]{1,0:T(8,128)(2,1)}, bf16[512,8192]{1,0:T(8,128)(2,1)}, bf16[512,8192]{1,0:T(8,128)(2,1)}) custom-call(bf16[512,2,8192]{2,1,0:T(2,128)(2,1)} %bitcast.25, bf16[128,144,2,128]{3,2,1,0:T(2,128)(2,1)} %pack_0.1.after_ref), custom_call_target="tpu_custom_call" | custom-call | flops 8589934592 | bytes 41943040 | tf_op jit(solution)/shard_map/tabulate/pallas_call | solution.py:188
  59.7 80.5 %all-to-all-done.1.arrived_ref = bf16[128,144,2,128]{3,2,1,0:T(2,128)(2,1)} async-done(((bf16[128,144,2,128]{3,2,1,0:T(2,128)(2,1)}), bf16[128,144,2,128]{3,2,1,0:T(2,128)(2,1)}, u32[]{:S(2)}, u32[]{:S(2)}) %all-to-all-start.1) | async-done | bytes 9437216 | tf_op jit(solution)/shard_map/all_to_all | solution.py:324
  140.2 11.6 %all-to-all-start = ((bf16[128,50,2,128]{3,2,1,0:T(2,128)(2,1)}), bf16[128,50,2,128]{3,2,1,0:T(2,128)(2,1)}, u32[]{:S(2)}, u32[]{:S(2)}) async-start(bf16[128,50,2,128]{3,2,1,0:T(2,128)(2,1)} %pack_1.1), calls=%async_computation | async-start | bytes 6553600 | tf_op jit(solution)/shard_map/all_to_all | solution.py:324
  151.9 0.0 copy-done.1
  151.9 0.2 convert_reduce_fusion
  152.1 16.1 %match_0.1.base_ref = f32[256,512]{1,0:T(8,128)} custom-call(bf16[128,144,2,128]{3,2,1,0:T(2,128)(2,1)} %all-to-all-done.1.arrived_ref, f32[1,8192]{1,0:T(1,128)} %weight_ref.3, bf16[512,8192]{1,0:T(8,128)(2,1)} %get-tuple-element.16.re_ref, bf16[512,8192]{1,0:T(8,128)(2,1)} %get-tuple-element.17.im_ref, bf16[512,8192]{1,0:T(8,128)(2,1)} %get-tuple-element.18.pw_ref), custom_call_target="tpu_custom_call" | custom-call | flops 4831838208 | bytes 28311552 | tf_op jit(solution)/shard_map/match_0/pallas_call | solution.py:291
  168.2 26.5 %all-to-all-done.arrived_ref.near_ref = bf16[128,50,2,128]{3,2,1,0:T(2,128)(2,1)} async-done(((bf16[128,50,2,128]{3,2,1,0:T(2,128)(2,1)}), bf16[128,50,2,128]{3,2,1,0:T(2,128)(2,1)}, u32[]{:S(2)}, u32[]{:S(2)}) %all-to-all-start) | async-done | bytes 3276832 | tf_op jit(solution)/shard_map/all_to_all | solution.py:324
  194.7 7.9 %match_1.1 = f32[128,2,128]{2,1,0:T(2,128)} custom-call(bf16[128,50,2,128]{3,2,1,0:T(2,128)(2,1)} %all-to-all-done.arrived_ref.near_ref, f32[1,8192]{1,0:T(1,128)} %weight_ref.3, bf16[512,8192]{1,0:T(8,128)(2,1)} %get-tuple-element.16.re_ref, bf16[512,8192]{1,0:T(8,128)(2,1)} %get-tuple-element.17.im_ref, bf16[512,8192]{1,0:T(8,128)(2,1)} %get-tuple-element.18.pw_ref, ...), custom_call_target="tpu_custom_call" | custom-call | flops 1677721600 | bytes 9830400 | tf_op jit(solution)/shard_map/match_1/pallas_call | solution.py:299
  202.6 4.5 %all-to-all-start.2 = ((f32[128,2,128]{2,1,0:T(2,128)}), f32[128,2,128]{2,1,0:T(2,128)S(1)}, u32[]{:S(2)}, u32[]{:S(2)}) async-start(f32[128,2,128]{2,1,0:T(2,128)} %match_1.1), calls=%async_computation.2 | async-start | bytes 262144 | tf_op jit(solution)/shard_map/all_to_all | solution.py:324
  207.1 0.1 add_bitcast_fusion
  207.2 9.8 %all-to-all-done.2 = f32[128,2,128]{2,1,0:T(2,128)S(1)} async-done(((f32[128,2,128]{2,1,0:T(2,128)}), f32[128,2,128]{2,1,0:T(2,128)S(1)}, u32[]{:S(2)}, u32[]{:S(2)}) %all-to-all-start.2) | async-done | bytes 131104 | tf_op jit(solution)/shard_map/all_to_all | solution.py:324
  217.0 0.3 fusion.1
  217.3 0.7 copy.9
  (2 shorter events, 0.0 us)
Async XLA Ops:
  10.9 11.9 %copy-start = (s32[32,4,128]{2,1,0:T(4,128)S(1)}, s32[32,4,128]{2,1,0:T(4,128)}, u32[]{:S(2)}) copy-start(s32[32,4,128]{2,1,0:T(4,128)} %param.11) | copy-start | bytes 196612
  10.9 129.3 %all-to-all-start.1 = ((bf16[128,144,2,128]{3,2,1,0:T(2,128)(2,1)}), bf16[128,144,2,128]{3,2,1,0:T(2,128)(2,1)}, u32[]{:S(2)}, u32[]{:S(2)}) async-start(bf16[128,144,2,128]{3,2,1,0:T(2,128)(2,1)} %pack_0.1.after_ref), calls=%async_computation.1 | async-start | bytes 18874368 | tf_op jit(solution)/shard_map/all_to_all | solution.py:324
  28.8 123.1 %copy-start.1 = (s32[4,32,1]{1,2,0:T(1,128)S(1)}, s32[4,32,1]{1,2,0:T(1,128)}, u32[]{:S(2)}) copy-start(s32[4,32,1]{1,2,0:T(1,128)} %param.10) | copy-start | bytes 1540
  140.2 54.5 %all-to-all-start = ((bf16[128,50,2,128]{3,2,1,0:T(2,128)(2,1)}), bf16[128,50,2,128]{3,2,1,0:T(2,128)(2,1)}, u32[]{:S(2)}, u32[]{:S(2)}) async-start(bf16[128,50,2,128]{3,2,1,0:T(2,128)(2,1)} %pack_1.1), calls=%async_computation | async-start | bytes 6553600 | tf_op jit(solution)/shard_map/all_to_all | solution.py:324
  202.6 14.4 %all-to-all-start.2 = ((f32[128,2,128]{2,1,0:T(2,128)}), f32[128,2,128]{2,1,0:T(2,128)S(1)}, u32[]{:S(2)}, u32[]{:S(2)}) async-start(f32[128,2,128]{2,1,0:T(2,128)} %match_1.1), calls=%async_computation.2 | async-start | bytes 262144 | tf_op jit(solution)/shard_map/all_to_all | solution.py:324

commit v5 on v4

--- a/solution.py
+++ b/solution.py
@@ -11,7 +11,7 @@
 PIX = 8192
 LANES = 128
 SLABS = PIX // LANES
-WIDTHS = (48, 16)
+WIDTHS = (32, 32)
 GROUP = 8
 NEAR = 128
 
@@ -284,7 +284,7 @@
             bytes_accessed=2 * depth * LANES * (rows + orients),
             transcendentals=0,
         ),
-        compiler_params=pltpu.CompilerParams(vmem_limit_bytes=63 * 2**20),
+        compiler_params=pltpu.CompilerParams(vmem_limit_bytes=48 * 2**20),
         name=f"match_{chunk}",
     )
     if base is None:

time: 218 us -> 214 us (0.982)
  waiting for transfers between devices: 117 us -> 111 us
  starting transfers between devices: 28.1 us -> 30.8 us
    all_to_all x3, waiting for transfers between devices: 117 us -> 111 us  [exchange(): lax.all_to_all(array, ('grp', 'orient'), split_axis=0, concat_axis=0, til...]
    pallas_call x1, Pallas kernels: 16.1 us -> 10.8 us  [match(): pl.pallas_call(match_first, in_specs=in_specs, out_specs=full, out_shape=...]
    pallas_call x1, Pallas kernels: 7.87 us -> 12.1 us  [match(): pl.pallas_call(match_last, in_specs=in_specs + [full, extra], out_specs=p...]
    all_to_all x3, starting transfers between devices: 28.1 us -> 30.8 us  [exchange(): lax.all_to_all(array, ('grp', 'orient'), split_axis=0, concat_axis=0, til...]
  transfers between devices with their start and end apart: 3 -> 3, of which waited for: 3 -> 3; matrix products, arithmetic and copies ran while one was open for 0% -> 0% of each run, Pallas kernels for 24% -> 23%
where the time goes in v5:
time: 214 us
  waiting for transfers between devices  111 us (52%)
  Pallas kernels  70.2 us (33%)
  starting transfers between devices  30.8 us (14%)
    all_to_all x3, waiting for transfers between devices, exchange(): lax.all_to_all(array, ('grp', 'orient'), split_axis=0, concat_axis=0, til...  111 us
    pallas_call x1, Pallas kernels, tabulate(): pl.pallas_call(table_kernel, grid=(orients // rows,), in_specs=[pl.BlockS...  31 us
    all_to_all x3, starting transfers between devices, exchange(): lax.all_to_all(array, ('grp', 'orient'), split_axis=0, concat_axis=0, til...  30.8 us
    pallas_call x2, Pallas kernels, pack(): pl.pallas_call(body, grid=(1,), in_specs=[whole(shifts), whole(home), pl....  16.2 us
    pallas_call x1, Pallas kernels, match(): pl.pallas_call(match_last, in_specs=in_specs + [full, extra], out_specs=p...  12.1 us
    pallas_call x1, Pallas kernels, match(): pl.pallas_call(match_first, in_specs=in_specs, out_specs=full, out_shape=...  10.8 us
  transfers between devices with their start and end apart: 3, of which 3 were waited for; matrix products, arithmetic and copies ran while one was open for 0% of the time, Pallas kernels for 23%

profile of v5, /device:TPU:1, one launch (start us, length us, event | category | flops | bytes accessed | tf_op | source)
XLA Modules:
  0.0 214.1 jit_solution(8632082603733527616)
XLA Ops:
  0.0 0.0 copy-start.1
  0.0 8.0 %pack_0.1.after_ref = bf16[128,96,2,128]{3,2,1,0:T(2,128)(2,1)} custom-call(s32[2,32]{1,0:T(2,128)} %bitcast.23, s32[4,32]{1,0:T(4,128)} %bitcast.19, bf16[32,2,8192]{2,1,0:T(2,128)(2,1)} %refs_2_.3, bf16[32,8192]{1,0:T(8,128)(2,1)} %refs_3_.3), custom_call_target="tpu_custom_call" | custom-call | flops 201326592 | bytes 7077888 | tf_op jit(solution)/shard_map/pack_0/pallas_call | solution.py:141
  8.0 11.9 %all-to-all-start.1 = ((bf16[128,96,2,128]{3,2,1,0:T(2,128)(2,1)}), bf16[128,96,2,128]{3,2,1,0:T(2,128)(2,1)}, u32[]{:S(2)}, u32[]{:S(2)}) async-start(bf16[128,96,2,128]{3,2,1,0:T(2,128)(2,1)} %pack_0.1.after_ref), calls=%async_computation.1 | async-start | bytes 12582912 | tf_op jit(solution)/shard_map/all_to_all | solution.py:324
  19.9 0.0 copy-done.1
  20.0 0.6 copy.12
  20.6 8.2 %pack_1.1 = bf16[128,98,2,128]{3,2,1,0:T(2,128)(2,1)} custom-call(s32[2,32]{1,0:T(2,128)} %bitcast.24, s32[4,32]{1,0:T(4,128)} %bitcast.20, bf16[32,2,8192]{2,1,0:T(2,128)(2,1)} %refs_2_.3, bf16[32,8192]{1,0:T(8,128)(2,1)} %refs_3_.3, s32[32,512]{1,0:T(8,128)} %bitcast.17), custom_call_target="tpu_custom_call" | custom-call | flops 205520896 | bytes 7225344 | tf_op jit(solution)/shard_map/pack_1/pallas_call | solution.py:141
  28.8 31.0 %tabulate.1 = (bf16[512,8192]{1,0:T(8,128)(2,1)}, bf16[512,8192]{1,0:T(8,128)(2,1)}, bf16[512,8192]{1,0:T(8,128)(2,1)}) custom-call(bf16[512,2,8192]{2,1,0:T(2,128)(2,1)} %bitcast.25, bf16[128,96,2,128]{3,2,1,0:T(2,128)(2,1)} %pack_0.1.after_ref), custom_call_target="tpu_custom_call" | custom-call | flops 8589934592 | bytes 41943040 | tf_op jit(solution)/shard_map/tabulate/pallas_call | solution.py:188
  59.8 0.0 copy-start.2
  59.8 0.0 copy-start
  59.8 35.6 %all-to-all-done.1.arrived_ref = bf16[128,96,2,128]{3,2,1,0:T(2,128)(2,1)} async-done(((bf16[128,96,2,128]{3,2,1,0:T(2,128)(2,1)}), bf16[128,96,2,128]{3,2,1,0:T(2,128)(2,1)}, u32[]{:S(2)}, u32[]{:S(2)}) %all-to-all-start.1) | async-done | bytes 6291488 | tf_op jit(solution)/shard_map/all_to_all | solution.py:324
  95.4 9.3 %all-to-all-start = ((bf16[128,98,2,128]{3,2,1,0:T(2,128)(2,1)}), bf16[128,98,2,128]{3,2,1,0:T(2,128)(2,1)}, u32[]{:S(2)}, u32[]{:S(2)}) async-start(bf16[128,98,2,128]{3,2,1,0:T(2,128)(2,1)} %pack_1.1), calls=%async_computation | async-start | bytes 12845056 | tf_op jit(solution)/shard_map/all_to_all | solution.py:324
  104.7 0.0 copy-done.2
  104.7 0.2 convert_reduce_fusion
  104.9 0.0 copy-done
  104.9 10.8 %match_0.1.base_ref = f32[256,512]{1,0:T(8,128)S(1)} custom-call(bf16[128,96,2,128]{3,2,1,0:T(2,128)(2,1)} %all-to-all-done.1.arrived_ref, f32[1,8192]{1,0:T(1,128)S(1)} %copy-done, bf16[512,8192]{1,0:T(8,128)(2,1)} %get-tuple-element.16.re_ref, bf16[512,8192]{1,0:T(8,128)(2,1)} %get-tuple-element.17.im_ref, bf16[512,8192]{1,0:T(8,128)(2,1)} %get-tuple-element.18.pw_ref), custom_call_target="tpu_custom_call" | custom-call | flops 3221225472 | bytes 18874368 | tf_op jit(solution)/shard_map/match_0/pallas_call | solution.py:291
  115.7 65.9 %all-to-all-done.arrived_ref.near_ref = bf16[128,98,2,128]{3,2,1,0:T(2,128)(2,1)} async-done(((bf16[128,98,2,128]{3,2,1,0:T(2,128)(2,1)}), bf16[128,98,2,128]{3,2,1,0:T(2,128)(2,1)}, u32[]{:S(2)}, u32[]{:S(2)}) %all-to-all-start) | async-done | bytes 6422560 | tf_op jit(solution)/shard_map/all_to_all | solution.py:324
  181.6 12.1 %match_1.1 = f32[128,2,128]{2,1,0:T(2,128)} custom-call(bf16[128,98,2,128]{3,2,1,0:T(2,128)(2,1)} %all-to-all-done.arrived_ref.near_ref, f32[1,8192]{1,0:T(1,128)S(1)} %copy-done, bf16[512,8192]{1,0:T(8,128)(2,1)} %get-tuple-element.16.re_ref, bf16[512,8192]{1,0:T(8,128)(2,1)} %get-tuple-element.17.im_ref, bf16[512,8192]{1,0:T(8,128)(2,1)} %get-tuple-element.18.pw_ref, ...), custom_call_target="tpu_custom_call" | custom-call | flops 3288334336 | bytes 19267584 | tf_op jit(solution)/shard_map/match_1/pallas_call | solution.py:299
  193.8 9.6 %all-to-all-start.2 = ((f32[128,2,128]{2,1,0:T(2,128)}), f32[128,2,128]{2,1,0:T(2,128)S(1)}, u32[]{:S(2)}, u32[]{:S(2)}) async-start(f32[128,2,128]{2,1,0:T(2,128)} %match_1.1), calls=%async_computation.2 | async-start | bytes 262144 | tf_op jit(solution)/shard_map/all_to_all | solution.py:324
  203.4 0.1 add_bitcast_fusion
  203.5 9.7 %all-to-all-done.2 = f32[128,2,128]{2,1,0:T(2,128)S(1)} async-done(((f32[128,2,128]{2,1,0:T(2,128)}), f32[128,2,128]{2,1,0:T(2,128)S(1)}, u32[]{:S(2)}, u32[]{:S(2)}) %all-to-all-start.2) | async-done | bytes 131104 | tf_op jit(solution)/shard_map/all_to_all | solution.py:324
  213.2 0.3 fusion.1
  213.4 0.7 copy.9
  (2 shorter events, 0.0 us)
Async XLA Ops:
  0.0 19.9 %copy-start.1 = (s32[32,4,128]{2,1,0:T(4,128)S(1)}, s32[32,4,128]{2,1,0:T(4,128)}, u32[]{:S(2)}) copy-start(s32[32,4,128]{2,1,0:T(4,128)} %param.11) | copy-start | bytes 196612
  8.0 87.3 %all-to-all-start.1 = ((bf16[128,96,2,128]{3,2,1,0:T(2,128)(2,1)}), bf16[128,96,2,128]{3,2,1,0:T(2,128)(2,1)}, u32[]{:S(2)}, u32[]{:S(2)}) async-start(bf16[128,96,2,128]{3,2,1,0:T(2,128)(2,1)} %pack_0.1.after_ref), calls=%async_computation.1 | async-start | bytes 12582912 | tf_op jit(solution)/shard_map/all_to_all | solution.py:324
  59.8 44.9 %copy-start.2 = (s32[4,32,1]{1,2,0:T(1,128)S(1)}, s32[4,32,1]{1,2,0:T(1,128)}, u32[]{:S(2)}) copy-start(s32[4,32,1]{1,2,0:T(1,128)} %param.10) | copy-start | bytes 1540
  59.8 45.1 %copy-start = (f32[1,8192]{1,0:T(1,128)S(1)}, f32[1,8192]{1,0:T(1,128)}, u32[]{:S(2)}) copy-start(f32[1,8192]{1,0:T(1,128)} %weight_ref.3) | copy-start | bytes 98308
  95.4 86.3 %all-to-all-start = ((bf16[128,98,2,128]{3,2,1,0:T(2,128)(2,1)}), bf16[128,98,2,128]{3,2,1,0:T(2,128)(2,1)}, u32[]{:S(2)}, u32[]{:S(2)}) async-start(bf16[128,98,2,128]{3,2,1,0:T(2,128)(2,1)} %pack_1.1), calls=%async_computation | async-start | bytes 12845056 | tf_op jit(solution)/shard_map/all_to_all | solution.py:324
  193.8 19.4 %all-to-all-start.2 = ((f32[128,2,128]{2,1,0:T(2,128)}), f32[128,2,128]{2,1,0:T(2,128)S(1)}, u32[]{:S(2)}, u32[]{:S(2)}) async-start(f32[128,2,128]{2,1,0:T(2,128)} %match_1.1), calls=%async_computation.2 | async-start | bytes 262144 | tf_op jit(solution)/shard_map/all_to_all | solution.py:324
